TPU v7x, 32 devices: a 4x4x1 block of a 4x4x8 slice. The times are simulated.
32 devices in a mesh: batch: 1 (over z), time: 4 (over y), region: 8 (over x, core).
Axes of the slice: x: 4, y: 4, z: 1, core: 2. Of those that a mesh axis runs over, the one named last changes fastest.
The devices are a block of a 4x4x8 slice.
Arguments:
- patches: bfloat16 [2048, 768], P(('batch', 'time', 'region'))
- enc_pos: bfloat16 [2048, 1024], P(('batch', 'time', 'region'))
- vis_mask: int32 [2048], P(('batch', 'time', 'region'))
- dec_pos: bfloat16 [2048, 512], P(('batch', 'time', 'region'))
- w_embed: bfloat16 [768, 1024], replicated
- b_embed: float32 [1024], replicated
- enc_vec: float32 [2, 12, 1024], replicated
- enc_wqkv: bfloat16 [2, 1024, 3, 16, 64], replicated
- enc_wo: bfloat16 [2, 16, 64, 1024], replicated
- enc_w1: bfloat16 [2, 1024, 4096], replicated
- enc_w2: bfloat16 [2, 4096, 1024], replicated
- enc_final: float32 [2, 1024], replicated
- w_dec_in: bfloat16 [1024, 512], replicated
- mask_token: bfloat16 [512], replicated
- dec_vec: float32 [2, 12, 512], replicated
- dec_wqkv: bfloat16 [2, 512, 3, 16, 32], replicated
- dec_wo: bfloat16 [2, 16, 32, 512], replicated
- dec_w1: bfloat16 [2, 512, 2048], replicated
- dec_w2: bfloat16 [2, 2048, 512], replicated
- dec_final: float32 [2, 512], replicated
- w_out: bfloat16 [512, 768], replicated
Outputs:
- output: float32 [2048, 768], P(('batch', 'time', 'region'))
All inputs are finite; a program needn't handle non-finite values.
Results may differ from a plain program's by a relative error of at most 0.016158.
Values are sent between devices in bfloat16 or wider.
A program may use at most 768 MiB of HBM per device.

v0:
```python
import functools
import jax
import jax.numpy as jnp
from jax import lax
from jax.sharding import PartitionSpec as P

KEEP_DIV = 8
LN_EPS = 1e-6
GROUP_AXES = ("time", "region")
TOKEN_AXES = ("batch", "time", "region")


def layer_norm(hidden, ln_gain, ln_shift):
    hid_f32 = hidden.astype(jnp.float32)
    mean_val = jnp.mean(hid_f32, axis=-1, keepdims=True)
    centered = hid_f32 - mean_val
    variance = jnp.mean(centered * centered, axis=-1, keepdims=True)
    return centered * lax.rsqrt(variance + LN_EPS) * ln_gain + ln_shift


def attend(query_rows, key_rows, value_rows, key_bias):
    head_dim = query_rows.shape[-1]
    scores = jnp.einsum("qhd,khd->hqk", query_rows, key_rows, preferred_element_type=jnp.float32) * (head_dim ** -0.5)
    if key_bias is not None:
        scores = scores + key_bias
    attn_probs = jax.nn.softmax(scores, axis=-1).astype(jnp.bfloat16)
    return jnp.einsum("hqk,khd->qhd", attn_probs, value_rows, preferred_element_type=jnp.float32).astype(jnp.bfloat16)


def run_block(hidden, vec_rows, w_qkv, w_o, w_one, w_two, gather_rows, key_bias):
    head_count, head_dim = w_qkv.shape[2], w_qkv.shape[3]
    normed = layer_norm(hidden, vec_rows[0], vec_rows[1]).astype(jnp.bfloat16)
    qkv_bias = jnp.stack([vec_rows[4], jnp.zeros_like(vec_rows[4]), vec_rows[5]]).reshape(1, 3, head_count, head_dim)
    qkv_rows = (jnp.einsum("nd,dche->nche", normed, w_qkv, preferred_element_type=jnp.float32) + qkv_bias).astype(jnp.bfloat16)
    key_rows = gather_rows(qkv_rows[:, 1])
    value_rows = gather_rows(qkv_rows[:, 2])
    attended = attend(qkv_rows[:, 0], key_rows, value_rows, key_bias)
    residual = (hidden.astype(jnp.float32) + jnp.einsum("nhe,hed->nd", attended, w_o, preferred_element_type=jnp.float32) + vec_rows[6]).astype(jnp.bfloat16)
    normed_mlp = layer_norm(residual, vec_rows[2], vec_rows[3]).astype(jnp.bfloat16)
    mlp_hidden = jax.nn.gelu(jnp.dot(normed_mlp, w_one, preferred_element_type=jnp.float32) + vec_rows[8:12].reshape(-1), approximate=False).astype(jnp.bfloat16)
    return (residual.astype(jnp.float32) + jnp.dot(mlp_hidden, w_two, preferred_element_type=jnp.float32) + vec_rows[7]).astype(jnp.bfloat16)


def solution(mesh):
    regions = mesh.shape["region"]
    skew_factor = min(4, regions)
    gather_group = functools.partial(lax.all_gather, axis_name=GROUP_AXES, axis=0, tiled=True)

    def local_step(patches, enc_pos, vis_mask, dec_pos, w_embed, b_embed, enc_vec, enc_wqkv, enc_wo, enc_w1, enc_w2, enc_final, w_dec_in, mask_token, dec_vec, dec_wqkv, dec_wo, dec_w1, dec_w2, dec_final, w_out):
        tokens_dev = patches.shape[0]
        vis_dev = tokens_dev // KEEP_DIV
        cap_rows = skew_factor * vis_dev
        enc_width = w_embed.shape[1]
        dec_width = w_dec_in.shape[1]
        region_pos = lax.axis_index("region")
        own_count = jnp.sum(vis_mask)
        counts = lax.all_gather(own_count[None], "region", axis=0, tiled=True)
        starts = jnp.cumsum(counts) - counts
        offset = starts[region_pos]
        slot_ids = jnp.arange(cap_rows, dtype=jnp.int32)
        local_rank = jnp.cumsum(vis_mask) - 1
        selector = ((local_rank[None, :] == slot_ids[:, None]) & (vis_mask[None, :] == 1)).astype(jnp.bfloat16)
        picked_patch = jnp.dot(selector, patches, preferred_element_type=jnp.float32).astype(jnp.bfloat16)
        picked_pos = jnp.dot(selector, enc_pos, preferred_element_type=jnp.float32)
        embedded = jnp.dot(picked_patch, w_embed, preferred_element_type=jnp.float32) + b_embed + picked_pos
        embedded = jnp.where((slot_ids < own_count)[:, None], embedded, 0.0).astype(jnp.bfloat16)
        rank_space = lax.dynamic_update_slice(jnp.zeros((regions * vis_dev + cap_rows, enc_width), jnp.bfloat16), embedded, (offset, 0))
        send_rows = rank_space[: regions * vis_dev].reshape(regions, vis_dev, enc_width)
        received = lax.all_to_all(send_rows, "region", 0, 0, tiled=True)
        hidden = jnp.sum(received, axis=0)
        for layer_idx in range(enc_vec.shape[0]):
            hidden = run_block(hidden, enc_vec[layer_idx], enc_wqkv[layer_idx], enc_wo[layer_idx], enc_w1[layer_idx], enc_w2[layer_idx], gather_group, None)
        latent = jnp.dot(layer_norm(hidden, enc_final[0], enc_final[1]).astype(jnp.bfloat16), w_dec_in, preferred_element_type=jnp.float32).astype(jnp.bfloat16)
        my_ranks = region_pos * vis_dev + jnp.arange(vis_dev, dtype=jnp.int32)
        from_source = (my_ranks[None, :] >= starts[:, None]) & (my_ranks[None, :] < (starts + counts)[:, None])
        back_rows = jnp.where(from_source[:, :, None], latent[None], jnp.zeros((), jnp.bfloat16))
        returned = lax.all_to_all(back_rows, "region", 0, 0, tiled=True)
        return_space = jnp.concatenate([returned.reshape(regions * vis_dev, dec_width), jnp.zeros((cap_rows, dec_width), jnp.bfloat16)], axis=0)
        own_latent = lax.dynamic_slice(return_space, (offset, 0), (cap_rows, dec_width))
        placed = jnp.einsum("ct,cd->td", selector, own_latent, preferred_element_type=jnp.float32)
        hidden = (jnp.where(vis_mask[:, None] == 1, placed, mask_token.astype(jnp.float32)) + dec_pos.astype(jnp.float32)).astype(jnp.bfloat16)
        for layer_idx in range(dec_vec.shape[0]):
            hidden = run_block(hidden, dec_vec[layer_idx], dec_wqkv[layer_idx], dec_wo[layer_idx], dec_w1[layer_idx], dec_w2[layer_idx], gather_group, None)
        return jnp.dot(layer_norm(hidden, dec_final[0], dec_final[1]).astype(jnp.bfloat16), w_out, preferred_element_type=jnp.float32)

    token_rows = P(TOKEN_AXES, None)
    token_flags = P(TOKEN_AXES)
    replicated = P()
    in_specs = (token_rows, token_rows, token_flags, token_rows) + (replicated,) * 17
    return jax.shard_map(local_step, mesh=mesh, in_specs=in_specs, out_specs=token_rows, check_vma=False)
```

profile of v0, /device:TPU:97, one launch (start us, length us, event | category | flops | bytes accessed | tf_op | source)
XLA Modules:
  0.0 473.2 jit_solution(11869926563829972643)
XLA Ops:
  6.6 0.8 broadcast_compare_fusion
  7.3 1.3 reduce_sum.237
  9.3 1.3 dynamic-slice
  10.6 1.4 dynamic-update-slice
  12.0 8.9 %all-reduce.1 = s32[8]{0:T(128)S(1)} all-reduce(s32[8]{0:T(128)S(1)} %dynamic-update-slice), channel_id=1, replica_groups=mesh['batch'=1,'time'=4,'region'=8] {'region'}, use_global_device_ids=true, to_apply=%add.1 | all-reduce | flops 8 | bytes 64
  24.7 1.4 convolution_add_fusion.3
  26.0 1.1 fusion.122
  28.4 5.5 %all-to-all-start = ((bf16[8,8,1024]{2,1,0:T(8,128)(2,1)}), bf16[8,8,1024]{2,1,0:T(8,128)(2,1)S(1)}, u32[]{:S(2)}, u32[]{:S(2)}) async-start(bf16[8,8,1024]{2,1,0:T(8,128)(2,1)} %slice_bitcast_fusion.4), calls=%async_computation | async-start | bytes 262144 | tf_op jit(solution)/shard_map/all_to_all | solution.py:69
  33.8 1.0 fusion.596
  34.8 0.9 fusion.597
  36.0 0.8 fusion.602
  36.7 1.5 fusion.600
  38.2 2.2 fusion.593
  41.3 5.3 %fusion.77 = bf16[8,3,16,64]{3,0,2,1:T(8,128)(2,1)S(1)} fusion(bf16[2,1024,3,16,64]{1,4,3,2,0:T(8,128)(2,1)} %param.28, f32[3,16,64]{2,1,0:T(8,128)S(1)} %get-tuple-element.66, bf16[8,1024]{1,0:T(8,128)(2,1)S(1)} %reduce_sum.238, f32[1024]{0:T(1024)S(1)} %bitcast.396, f32[1024]{0:T(1024)S(1)} %bitcast.397, f32[8]{0:T(128)S(1)} %add_rsqrt_fusion.9, ...), kind=kOutput, calls=%fused_computation.67 | convolution fusion | flops 50429952 | bytes 6377536 | tf_op jit(solution)/shard_map/nd,dche->nche/dot_general | solution.py:34
  46.7 32.7 %all-gather.1 = bf16[256,1,16,64]{3,0,2,1:T(8,128)(2,1)S(1)} all-gather(bf16[8,1,16,64]{3,0,2,1:T(8,128)(2,1)S(1)} %get-tuple-element.39), channel_id=3, replica_groups=mesh['batch'=1,'time'=4,'region'=8] {'time','region'}, dimensions={0}, use_global_device_ids=true | all-gather | bytes 540672 | tf_op jit(solution)/shard_map/all_gather | solution.py:35
  80.0 35.5 %all-gather = bf16[256,1,16,64]{3,0,2,1:T(8,128)(2,1)} all-gather(bf16[8,1,16,64]{3,0,2,1:T(8,128)(2,1)S(1)} %get-tuple-element.40), channel_id=2, replica_groups=mesh['batch'=1,'time'=4,'region'=8] {'time','region'}, dimensions={0}, use_global_device_ids=true | all-gather | bytes 540672 | tf_op jit(solution)/shard_map/all_gather | solution.py:36
  115.5 2.7 fusion.605
  118.4 7.2 %fusion.608 = (f32[8]{0:T(128)S(1)}, f32[8,1024]{1,0:T(8,128)S(1)}) fusion(f32[1024]{0:T(1024)S(1)} %bitcast.410, f32[8,1024]{1,0:T(8,128)S(1)} %get-tuple-element.68, bf16[2,4096,1024]{2,1,0:T(8,128)(2,1)} %param.31, bf16[2,1024,4096]{2,1,0:T(8,128)(2,1)} %param.30, f32[4096]{0:T(1024)S(1)} %bitcast.393, f32[1024]{0:T(1024)S(1)} %bitcast.411, ...), kind=kOutput, calls=%fused_computation.599 | convolution fusion | flops 136462336 | bytes 16905248 | tf_op jit(solution)/shard_map/dot_general | solution.py:41
  125.9 5.3 %fusion.74 = bf16[8,3,16,64]{3,0,2,1:T(8,128)(2,1)S(1)} fusion(bf16[2,1024,3,16,64]{1,4,3,2,0:T(8,128)(2,1)} %param.28, f32[3,16,64]{2,1,0:T(8,128)S(1)} %get-tuple-element.65, f32[8,1024]{1,0:T(8,128)S(1)} %get-tuple-element.70, f32[1024]{0:T(1024)S(1)} %bitcast.394, f32[1024]{0:T(1024)S(1)} %bitcast.395, f32[8]{0:T(128)S(1)} %add_rsqrt_fusion.7, ...), kind=kOutput, calls=%fused_computation.66 | convolution fusion | flops 50421760 | bytes 6393920 | tf_op jit(solution)/shard_map/nd,dche->nche/dot_general | solution.py:34
  131.3 35.6 %all-gather.3 = bf16[256,1,16,64]{3,0,2,1:T(8,128)(2,1)S(1)} all-gather(bf16[8,1,16,64]{3,0,2,1:T(8,128)(2,1)S(1)} %get-tuple-element.37), channel_id=5, replica_groups=mesh['batch'=1,'time'=4,'region'=8] {'time','region'}, dimensions={0}, use_global_device_ids=true | all-gather | bytes 540672 | tf_op jit(solution)/shard_map/all_gather | solution.py:35
  167.5 35.7 %all-gather.2 = bf16[256,1,16,64]{3,0,2,1:T(8,128)(2,1)} all-gather(bf16[8,1,16,64]{3,0,2,1:T(8,128)(2,1)S(1)} %get-tuple-element.38), channel_id=4, replica_groups=mesh['batch'=1,'time'=4,'region'=8] {'time','region'}, dimensions={0}, use_global_device_ids=true | all-gather | bytes 540672 | tf_op jit(solution)/shard_map/all_gather | solution.py:36
  203.1 2.7 fusion.612
  206.1 7.3 %fusion.615 = (f32[8]{0:T(128)S(1)}, f32[8,1024]{1,0:T(8,128)S(1)}) fusion(f32[1024]{0:T(1024)S(1)} %bitcast.408, f32[8,1024]{1,0:T(8,128)S(1)} %get-tuple-element.72, bf16[2,4096,1024]{2,1,0:T(8,128)(2,1)} %param.31, bf16[2,1024,4096]{2,1,0:T(8,128)(2,1)} %param.30, f32[4096]{0:T(1024)S(1)} %bitcast.392, f32[1024]{0:T(1024)S(1)} %bitcast.407, ...), kind=kOutput, calls=%fused_computation.602 | convolution fusion | flops 136462336 | bytes 16905248 | tf_op jit(solution)/shard_map/dot_general | solution.py:41
  213.6 1.5 convolution_convert_fusion.3
  215.8 10.9 %all-to-all-start.1 = ((bf16[8,8,512]{2,1,0:T(8,128)(2,1)}), bf16[8,8,512]{2,1,0:T(8,128)(2,1)S(1)}, u32[]{:S(2)}, u32[]{:S(2)}) async-start(bf16[8,8,512]{2,1,0:T(8,128)(2,1)} %broadcast_select_fusion), calls=%async_computation.1 | async-start | bytes 131072 | tf_op jit(solution)/shard_map/all_to_all | solution.py:77
  226.8 4.6 all-to-all-done.1
  232.9 0.9 copy.35
  233.9 0.9 copy.33
  235.0 0.8 fusion.601
  235.8 43.8 %all-gather.15.cloned.1.call-done = bf16[2048,1,16,32]{3,2,1,0:T(8,128)(2,1)} async-done(((bf16[64,1,16,32]{3,2,1,0:T(8,128)(2,1)}), bf16[2048,1,16,32]{3,2,1,0:T(8,128)(2,1)}) %all-gather.15.cloned.1.call-update) | async-done | bytes 2097168 | tf_op jit(solution)/shard_map/all_gather | solution.py:35
  279.6 9.3 %copy.36 = bf16[2048,1,16,32]{0,3,2,1:T(8,128)(2,1)} copy(bf16[2048,1,16,32]{3,2,1,0:T(8,128)(2,1)} %all-gather.15.cloned.1.call-done) | data formatting | bytes 4194304 | tf_op jit(solution)/shard_map/all_gather | solution.py:35
  288.9 2.9 fusion.47
  291.8 4.2 fusion.619
  296.0 32.5 %all-gather.13.cloned.1.call-done = bf16[2048,1,16,32]{3,2,1,0:T(8,128)(2,1)} async-done(((bf16[64,1,16,32]{3,2,1,0:T(8,128)(2,1)}), bf16[2048,1,16,32]{3,2,1,0:T(8,128)(2,1)}) %all-gather.13.cloned.1.call-update) | async-done | bytes 2097168 | tf_op jit(solution)/shard_map/all_gather | solution.py:36
  328.6 9.3 %copy.34 = bf16[2048,1,16,32]{0,3,2,1:T(8,128)(2,1)} copy(bf16[2048,1,16,32]{3,2,1,0:T(8,128)(2,1)} %all-gather.13.cloned.1.call-done) | data formatting | bytes 4194304 | tf_op jit(solution)/shard_map/all_gather | solution.py:36
  337.9 5.6 %fusion.620 = (f32[64]{0:T(128)S(1)}, f32[64,512]{1,0:T(8,128)S(1)}) fusion(f32[512]{0:T(512)S(1)} %bitcast.421, f32[64,512]{1,0:T(8,128)S(1)} %get-tuple-element.76, bf16[2,16,32,512]{3,2,1,0:T(8,128)(2,1)S(1)} %copy-done.9, f32[16,64,2048]{2,1,0:T(8,128)} %get-tuple-element.78, f32[16,64]{1,0:T(8,128)S(1)} %get-tuple-element.77, ...), kind=kOutput, calls=%fused_computation.605 | convolution fusion | flops 172163008 | bytes 11282688 | tf_op jit(solution)/shard_map/nhe,hed->nd/dot_general | solution.py:38
  343.8 4.2 fusion.623
  349.1 0.9 copy.39
  350.4 1.0 copy.37
  351.5 45.7 %all-gather.19.cloned.1.call-done = bf16[2048,1,16,32]{3,2,1,0:T(8,128)(2,1)} async-done(((bf16[64,1,16,32]{3,2,1,0:T(8,128)(2,1)}), bf16[2048,1,16,32]{3,2,1,0:T(8,128)(2,1)}) %all-gather.19.cloned.1.call-update) | async-done | bytes 2097168 | tf_op jit(solution)/shard_map/all_gather | solution.py:35
  397.1 9.3 %copy.40 = bf16[2048,1,16,32]{0,3,2,1:T(8,128)(2,1)} copy(bf16[2048,1,16,32]{3,2,1,0:T(8,128)(2,1)} %all-gather.19.cloned.1.call-done) | data formatting | bytes 4194304 | tf_op jit(solution)/shard_map/all_gather | solution.py:35
  406.5 2.9 fusion.41
  409.3 4.2 fusion.626
  413.6 32.4 %all-gather.17.cloned.1.call-done = bf16[2048,1,16,32]{3,2,1,0:T(8,128)(2,1)} async-done(((bf16[64,1,16,32]{3,2,1,0:T(8,128)(2,1)}), bf16[2048,1,16,32]{3,2,1,0:T(8,128)(2,1)}) %all-gather.17.cloned.1.call-update) | async-done | bytes 2097168 | tf_op jit(solution)/shard_map/all_gather | solution.py:36
  446.0 9.3 %copy.38 = bf16[2048,1,16,32]{0,3,2,1:T(8,128)(2,1)} copy(bf16[2048,1,16,32]{3,2,1,0:T(8,128)(2,1)} %all-gather.17.cloned.1.call-done) | data formatting | bytes 4194304 | tf_op jit(solution)/shard_map/all_gather | solution.py:36
  455.3 5.6 %fusion.627 = (f32[64]{0:T(128)S(1)}, f32[64,512]{1,0:T(8,128)S(1)}) fusion(f32[512]{0:T(512)S(1)} %bitcast.417, f32[64,512]{1,0:T(8,128)S(1)} %get-tuple-element.82, bf16[2,16,32,512]{3,2,1,0:T(8,128)(2,1)S(1)} %copy-done.10, f32[16,64,2048]{2,1,0:T(8,128)} %get-tuple-element.84, f32[16,64]{1,0:T(8,128)S(1)} %get-tuple-element.83, ...), kind=kOutput, calls=%fused_computation.608 | convolution fusion | flops 172163008 | bytes 11282688 | tf_op jit(solution)/shard_map/nhe,hed->nd/dot_general | solution.py:38
  461.1 4.3 fusion.630
  465.7 1.0 fusion.323
  (103 shorter events, 11.4 us)
Async XLA Ops:
  6.5 18.1 %copy-start = (bf16[768,1024]{1,0:T(8,128)(2,1)S(1)}, bf16[768,1024]{1,0:T(8,128)(2,1)}, u32[]{:S(2)}) copy-start(bf16[768,1024]{1,0:T(8,128)(2,1)} %param.25) | copy-start | bytes 4718596
  28.4 12.6 %all-to-all-start = ((bf16[8,8,1024]{2,1,0:T(8,128)(2,1)}), bf16[8,8,1024]{2,1,0:T(8,128)(2,1)S(1)}, u32[]{:S(2)}, u32[]{:S(2)}) async-start(bf16[8,8,1024]{2,1,0:T(8,128)(2,1)} %slice_bitcast_fusion.4), calls=%async_computation | async-start | bytes 262144 | tf_op jit(solution)/shard_map/all_to_all | solution.py:69
  206.1 20.7 %copy-start.8 = (bf16[512]{0:T(512)(128)(2,1)S(1)}, bf16[512]{0:T(512)(128)(2,1)}, u32[]{:S(2)}) copy-start(bf16[512]{0:T(512)(128)(2,1)} %param.34) | copy-start | bytes 3076
  206.1 25.3 %copy-start.3 = (bf16[64,512]{1,0:T(8,128)(2,1)S(1)}, bf16[64,512]{1,0:T(8,128)(2,1)}, u32[]{:S(2)}) copy-start(bf16[64,512]{1,0:T(8,128)(2,1)} %param.24) | copy-start | bytes 196612
  215.8 15.6 %all-to-all-start.1 = ((bf16[8,8,512]{2,1,0:T(8,128)(2,1)}), bf16[8,8,512]{2,1,0:T(8,128)(2,1)S(1)}, u32[]{:S(2)}, u32[]{:S(2)}) async-start(bf16[8,8,512]{2,1,0:T(8,128)(2,1)} %broadcast_select_fusion), calls=%async_computation.1 | async-start | bytes 131072 | tf_op jit(solution)/shard_map/all_to_all | solution.py:77
  226.7 52.9 %all-gather.15.cloned.1.call-start = ((), (), s32[]{:S(2)}) async-start(), calls=%async_computation.3 | async-start | bytes 8650752 | tf_op jit(solution)/shard_map/all_gather | solution.py:35
  233.9 94.7 %all-gather.13.cloned.1.call-start = ((), (), s32[]{:S(2)}) async-start(), calls=%async_computation.2 | async-start | bytes 8650752 | tf_op jit(solution)/shard_map/all_gather | solution.py:36
  234.9 162.2 %all-gather.19.cloned.1.call-start = ((), (), s32[]{:S(2)}) async-start(), calls=%async_computation.5 | async-start | bytes 8650752 | tf_op jit(solution)/shard_map/all_gather | solution.py:35
  296.0 41.9 %copy-start.7 = (f32[1,1,512]{2,0,1:T(1,128)S(1)}, f32[1,1,512]{2,0,1:T(1,128)}, u32[]{:S(2)}) copy-start(f32[1,1,512]{2,0,1:T(1,128)} %get-tuple-element.52) | copy-start | bytes 6148
  296.0 41.9 %copy-start.9 = (bf16[2,16,32,512]{3,2,1,0:T(8,128)(2,1)S(1)}, bf16[2,16,32,512]{3,2,1,0:T(8,128)(2,1)}, u32[]{:S(2)}) copy-start(bf16[2,16,32,512]{3,2,1,0:T(8,128)(2,1)} %param.37) | copy-start | bytes 3145732
  337.9 5.8 %copy-start.5 = (f32[1,1,512]{2,0,1:T(1,128)S(1)}, f32[1,1,512]{2,0,1:T(1,128)}, u32[]{:S(2)}) copy-start(f32[1,1,512]{2,0,1:T(1,128)} %get-tuple-element.50) | copy-start | bytes 6148
  337.9 5.8 %copy-start.6 = (f32[1,1,512]{2,0,1:T(1,128)S(1)}, f32[1,1,512]{2,0,1:T(1,128)}, u32[]{:S(2)}) copy-start(f32[1,1,512]{2,0,1:T(1,128)} %get-tuple-element.51) | copy-start | bytes 6148
  343.8 7.7 %copy-start.4 = (f32[2,512]{1,0:T(2,128)S(1)}, f32[2,512]{1,0:T(2,128)}, u32[]{:S(2)}) copy-start(f32[2,512]{1,0:T(2,128)} %param.40) | copy-start | bytes 12292
  350.1 95.8 %all-gather.17.cloned.1.call-start = ((), (), s32[]{:S(2)}) async-start(), calls=%async_computation.4 | async-start | bytes 8650752 | tf_op jit(solution)/shard_map/all_gather | solution.py:36
  413.6 41.8 %copy-start.10 = (bf16[2,16,32,512]{3,2,1,0:T(8,128)(2,1)S(1)}, bf16[2,16,32,512]{3,2,1,0:T(8,128)(2,1)}, u32[]{:S(2)}) copy-start(bf16[2,16,32,512]{3,2,1,0:T(8,128)(2,1)} %param.37) | copy-start | bytes 3145732
  461.1 5.6 %copy-start.1 = (bf16[768,1024]{1,0:T(8,128)(2,1)S(1)}, bf16[768,1024]{1,0:T(8,128)(2,1)}, u32[]{:S(2)}) copy-start(bf16[768,1024]{1,0:T(8,128)(2,1)} %param.25) | copy-start | bytes 4718596
  461.1 4.6 copy-start.2
Sparse Core Ops, SparseCore 0:
  234.0 45.5 all-gather.14
  281.7 46.8 all-gather.12
  350.2 46.8 all-gather.18
  399.1 46.8 all-gather.16
where the time goes:
time: 475 us; the launch traced here: 473 us
  waiting for transfers between devices  159 us (33%)
  blocking collectives  148 us (31%)
  matrix products  63.3 us (13%)
  local copies, waits for them, and re-layouts  54.4 us (11%)
  starting transfers between devices  16.8 us (4%)
  other arithmetic  15.6 us (3%)
  between operations  15.6 us (3%)
    all_gather x2, waiting for transfers between devices, run_block(): key_rows = gather_rows(qkv_rows[:, 1])  89.5 us
    all_gather x2, blocking collectives, run_block(): value_rows = gather_rows(qkv_rows[:, 2])  71.1 us
    all_gather x2, blocking collectives, run_block(): key_rows = gather_rows(qkv_rows[:, 1])  68.4 us
    all_gather x2, waiting for transfers between devices, run_block(): value_rows = gather_rows(qkv_rows[:, 2])  65 us
    dot_general x4, matrix products, run_block(): jnp.dot(mlp_hidden, w_two, preferred_element_type=jnp.float32)  23 us
    all_gather x2, local copies, waits for them, and re-layouts, run_block(): key_rows = gather_rows(qkv_rows[:, 1])  18.7 us
    all_gather x2, local copies, waits for them, and re-layouts, run_block(): value_rows = gather_rows(qkv_rows[:, 2])  18.7 us
    dot_general x4, matrix products, run_block(): jnp.einsum('nhe,hed->nd', attended, w_o, preferred_element_type=jnp.float32)  16.6 us
  transfers between devices with their start and end apart: 6, of which 5 were waited for; matrix products, arithmetic and copies ran while one was open for 9% of the time, Pallas kernels for 0%

commit v1 on v0

v1 whole, which is shorter than its diff:
```python
import functools
import jax
import jax.numpy as jnp
from jax import lax
from jax.experimental import pallas as pl
from jax.experimental.pallas import tpu as pltpu
from jax.sharding import PartitionSpec as P

KEEP_DIV = 8
LN_EPS = 1e-6
CORES = 2
TOKEN_AXES = ("batch", "time", "region")
MESH_ID = pl.DeviceIdType.MESH
F32 = jnp.float32
BF16 = jnp.bfloat16
LOG2E = 1.4426950408889634


def mm(lhs, rhs):
    return jnp.dot(lhs, rhs, preferred_element_type=F32)


def mm_t(lhs, rhs):
    return lax.dot_general(lhs, rhs, (((1,), (1,)), ((), ())), preferred_element_type=F32)


def norm(rows, gain, shift):
    rows = rows.astype(F32)
    centered = rows - jnp.mean(rows, axis=-1, keepdims=True)
    variance = jnp.mean(centered * centered, axis=-1, keepdims=True)
    return (centered * lax.rsqrt(variance + LN_EPS) * gain + shift).astype(BF16)


def gelu(val):
    return 0.5 * val * (1.0 + lax.erf(val * 0.7071067811865476))


def loop(count, body):
    lax.fori_loop(0, count, lambda i, c: (body(i), c)[1], 0)


def blk(i, size):
    return pl.ds(pl.multiple_of(i * size, size), size)


def column_of(row, lanes):
    return jnp.broadcast_to(row, (lanes, row.shape[1])).T


def head_rows(q_rows, heads):
    lanes = q_rows.shape[1]
    head = lax.broadcasted_iota(jnp.int32, q_rows.shape, 1) // (lanes // heads)
    return jnp.concatenate([jnp.where(head == h, q_rows, jnp.zeros_like(q_rows)) for h in range(heads)], axis=0)


def unstack_heads(out_t, heads):
    out = out_t.T
    rows = out.shape[0] // heads
    head = lax.broadcasted_iota(jnp.int32, (rows, out.shape[1]), 1) // (out.shape[1] // heads)
    total = jnp.where(head == 0, out[:rows], 0.0)
    for h in range(1, heads):
        total = total + jnp.where(head == h, out[h * rows:(h + 1) * rows], 0.0)
    return total


def kernel(nt, nr, patches, enc_pos, vis, dec_pos, b_embed, evec, efin, mtok, dvec, dfin,
           w_embed, wqkv, wo, w1, w2, w_dec, dqkv, dwo, dw1, dw2, w_out,
           out,
           X0, X1, Y0, Y1, Z0, SL, MT, MB, E, H1, H2, A, Q, K, VT, ATT, HM, Z, ZT, DP, A2, S, PR, HD,
           wsem, s_e, r_e, s_g, r_g, s_h, r_h):
    t = lax.axis_index("time")
    r = lax.axis_index("region")
    nx = nr // CORES
    x, core = r // CORES, lax.rem(r, CORES)
    partner = r + 1 - 2 * core
    tok = patches.shape[0]
    slots = SL.shape[1]
    vis_blk = E.shape[0] // nt
    ed, dd = E.shape[1], dec_pos.shape[1]
    nvis = E.shape[0]

    def xpeer(dx):
        return lax.rem(x + dx, nx) * CORES + core

    def tpeer(dy):
        return lax.rem(t + dy, nt)

    def xsrc(dx):
        return lax.rem(x + nx - dx, nx) * CORES + core

    def tsrc(dy):
        return lax.rem(t + nt - dy, nt)

    def rcopy(src, dst, ssem, rsem, tt, rr):
        return pltpu.make_async_remote_copy(src_ref=src, dst_ref=dst, send_sem=ssem, recv_sem=rsem,
                                            device_id={"time": tt, "region": rr}, device_id_type=MESH_ID)

    def load(src, dst, i):
        return pltpu.make_async_copy(src, dst, wsem.at[i])

    ld_embed = load(w_embed, Y1.at[0:w_embed.shape[0], 0:ed], 0)
    ld_embed.start()

    barrier = pltpu.get_barrier_semaphore()
    peers = [(t, partner)] + [(t, xpeer(d)) for d in range(1, nx)] + [(tpeer(d), r) for d in range(1, nt)]
    for tt, rr in peers:
        pl.semaphore_signal(barrier, inc=1, device_id={"time": tt, "region": rr}, device_id_type=MESH_ID)

    mask_row = vis[...].astype(F32)
    mask_pad = jnp.concatenate([mask_row, jnp.zeros((1, 128 - tok), F32)], axis=1)
    MT[r] = jnp.broadcast_to(mask_pad, (8, 128))
    tri = (lax.broadcasted_iota(jnp.int32, (128, 128), 0) < lax.broadcasted_iota(jnp.int32, (128, 128), 1)).astype(BF16)
    local_rank = mm(jnp.broadcast_to(mask_pad, (8, 128)).astype(BF16), tri)[0:1, 0:tok]
    slot_id = lax.broadcasted_iota(jnp.int32, (slots, tok), 0).astype(F32)
    selector = jnp.where((local_rank == slot_id) & (mask_row == 1.0), 1.0, 0.0).astype(BF16)

    ld_embed.wait()
    qkv_w, d_w = 3 * ed, 3 * dd
    ld_a = [load(wqkv.at[0], X0.at[0:qkv_w], 1), load(wo.at[0], X0.at[qkv_w:qkv_w + ed], 2)]
    ld_b = [load(w1.at[0], Y0, 3), load(w2.at[0], Z0, 4)]
    ld_c = [load(wqkv.at[1], X1.at[0:qkv_w], 5), load(wo.at[1], X1.at[qkv_w:qkv_w + ed], 6)]
    for cp in ld_a + ld_b + ld_c:
        cp.start()

    def embed_cols(j):
        cols = blk(j, 256)
        emb = (mm(patches[...], Y1[0:patches.shape[1], cols]) + b_embed[:, cols] + enc_pos[:, cols].astype(F32)).astype(BF16)
        SL[r, :, cols] = mm(selector, emb).astype(BF16)

    loop(ed // 256, embed_cols)
    ld_d = load(w1.at[1], Y1, 7)
    ld_d.start()
    pl.semaphore_wait(barrier, len(peers))

    st = []
    for i, rr in enumerate([partner] + [xpeer(d) for d in range(1, nx)]):
        st.append(rcopy(SL.at[r], SL.at[r], s_e.at[i], r_e.at[i], t, rr))
        st.append(rcopy(MT.at[r], MT.at[r], s_e.at[8 + i], r_e.at[8 + i], t, rr))
    for cp in st:
        cp.start()
    fw = []
    for d in range(1, nx):
        src = xsrc(d)
        rcopy(SL.at[src], SL.at[src], s_e.at[d], r_e.at[d], t, r).wait_recv()
        rcopy(MT.at[src], MT.at[src], s_e.at[8 + d], r_e.at[8 + d], t, r).wait_recv()
        one = rcopy(SL.at[src], SL.at[src], s_e.at[16 + d], r_e.at[16 + d], t, partner)
        two = rcopy(MT.at[src], MT.at[src], s_e.at[24 + d], r_e.at[24 + d], t, partner)
        one.start()
        two.start()
        fw += [one, two]
    rcopy(SL.at[partner], SL.at[partner], s_e.at[0], r_e.at[0], t, r).wait_recv()
    rcopy(MT.at[partner], MT.at[partner], s_e.at[8], r_e.at[8], t, r).wait_recv()
    for cp in fw:
        cp.wait_recv()

    mask_all = jnp.concatenate([MT[d, 0:1, :] for d in range(nr)], axis=0)
    MB[t] = mask_all
    counts = jnp.sum(mask_all, axis=1, keepdims=True)
    lane_dev = lax.broadcasted_iota(jnp.int32, (nr, nr * slots), 1) // slots
    sub_dev = lax.broadcasted_iota(jnp.int32, (nr, nr * slots), 0)
    lane_cnt = jnp.sum(jnp.where(lane_dev == sub_dev, counts, 0.0), axis=0, keepdims=True)
    lane_off = jnp.sum(jnp.where(sub_dev < lane_dev, counts, 0.0), axis=0, keepdims=True)
    lane_slot = lax.rem(lax.broadcasted_iota(jnp.int32, (1, nr * slots), 1), slots).astype(F32)
    target = jnp.where(lane_slot < lane_cnt, lane_off + lane_slot, -1.0)
    rank_id = lax.broadcasted_iota(jnp.int32, (vis_blk, nr * slots), 0).astype(F32)
    compact = jnp.where(target == rank_id, 1.0, 0.0).astype(BF16)
    my_rows = blk(t, vis_blk)

    def compact_cols(j):
        cols = blk(j, 256)
        E[my_rows, cols] = mm(compact, SL[:, :, cols].reshape(nr * slots, 256)).astype(BF16)

    loop(ed // 256, compact_cols)

    half = vis_blk // CORES
    st2 = []
    for d in range(1, nt):
        rows = pl.ds(pl.multiple_of(t * vis_blk + core * half, half), half)
        st2.append(rcopy(E.at[rows], E.at[rows], s_e.at[32 + d], r_e.at[32 + d], tpeer(d), r))
        st2.append(rcopy(MB.at[t], MB.at[t], s_e.at[40 + d], r_e.at[40 + d], tpeer(d), r))
    for cp in st2:
        cp.start()
    DP[t, r] = dec_pos[...]

    def gather(buf, ss, rs):
        hw = dd // 2
        first, second, third = [], [], []

        def step1():
            first.append(rcopy(buf.at[t, r], buf.at[t, r], ss.at[0], rs.at[0], t, partner))
            for d in range(1, nt):
                first.append(rcopy(buf.at[t, r], buf.at[t, r], ss.at[d], rs.at[d], tpeer(d), r))
            for d in range(1, nx):
                first.append(rcopy(buf.at[t, r], buf.at[t, r], ss.at[4 + d], rs.at[4 + d], t, xpeer(d)))
            for cp in first:
                cp.start()

        def to_partner(ref, i):
            cp = rcopy(ref, ref, ss.at[i], rs.at[i], t, partner)
            cp.start()
            third.append(cp)

        def step2():
            for d in range(1, max(nt, nx)):
                if d < nt:
                    src = tsrc(d)
                    rcopy(buf.at[src, r], buf.at[src, r], ss.at[d], rs.at[d], t, r).wait_recv()
                    for e in range(1, nx):
                        i = 8 + d * 4 + e
                        half_ref = buf.at[src, r, :, 0:hw]
                        cp = rcopy(half_ref, half_ref, ss.at[i], rs.at[i], t, xpeer(e))
                        cp.start()
                        second.append(cp)
                    to_partner(buf.at[src, r], 40 + d * 4)
                if d < nx:
                    src = xsrc(d)
                    rcopy(buf.at[t, src], buf.at[t, src], ss.at[4 + d], rs.at[4 + d], t, r).wait_recv()
                    for e in range(1, nt):
                        i = 24 + d * 4 + e
                        half_ref = buf.at[t, src, :, hw:dd]
                        cp = rcopy(half_ref, half_ref, ss.at[i], rs.at[i], tpeer(e), r)
                        cp.start()
                        second.append(cp)
                    to_partner(buf.at[t, src], 40 + d)

        def step3():
            for d in range(1, nt):
                for e in range(1, nx):
                    low = buf.at[tsrc(d), xsrc(e), :, 0:hw]
                    high = buf.at[tsrc(d), xsrc(e), :, hw:dd]
                    rcopy(low, low, ss.at[8 + d * 4 + e], rs.at[8 + d * 4 + e], t, r).wait_recv()
                    rcopy(high, high, ss.at[24 + e * 4 + d], rs.at[24 + e * 4 + d], t, r).wait_recv()
                    to_partner(buf.at[tsrc(d), xsrc(e)], 40 + d * 4 + e)

        def finish():
            rcopy(buf.at[t, partner], buf.at[t, partner], ss.at[0], rs.at[0], t, r).wait_recv()
            for cp in third:
                cp.wait_recv()

        def drain():
            for cp in first + second + third:
                cp.wait_send()

        return step1, step2, step3, finish, drain

    g1 = gather(DP, s_g, r_g)
    g1[0]()

    fw2 = []
    for d in range(1, nt):
        rows = pl.ds(pl.multiple_of(tsrc(d) * vis_blk + core * half, half), half)
        rcopy(E.at[rows], E.at[rows], s_e.at[32 + d], r_e.at[32 + d], t, r).wait_recv()
        cp = rcopy(E.at[rows], E.at[rows], s_e.at[48 + d], r_e.at[48 + d], t, partner)
        cp.start()
        fw2.append(cp)
        rcopy(MB.at[tsrc(d)], MB.at[tsrc(d)], s_e.at[40 + d], r_e.at[40 + d], t, r).wait_recv()
    for d in range(1, nt):
        rows = pl.ds(pl.multiple_of(tsrc(d) * vis_blk + (1 - core) * half, half), half)
        rcopy(E.at[rows], E.at[rows], s_e.at[48 + d], r_e.at[48 + d], t, r).wait_recv()

    def norm_rows(src, dst, count, gain, shift, start=0, step=32):
        def body(i):
            rows = pl.ds(pl.multiple_of(start + i * step, step), step)
            dst[blk(i, step), :] = norm(src[rows, :], gain, shift)
        loop(count // step, body)

    def project(dst, rows_n, src_rows, w, w_row, bias):
        def body(j):
            cols = blk(j, 512)
            acc = mm_t(A[src_rows, :], w[pl.ds(pl.multiple_of(w_row + j * 512, 512), 512), :])
            if bias is not None:
                acc = acc + bias(cols)
            dst[0:rows_n, cols] = acc.astype(BF16)
        loop(ed // 512, body)

    def enc_layer(layer, w_a, w_up, w_down, src, rows_n, start, wait_down):
        def vec(i):
            return evec[i, layer:layer + 1, :]

        norm_rows(src, A, nvis, vec(0), vec(1))
        q_rows = pl.ds(pl.multiple_of(start, rows_n), rows_n)
        project(Q, rows_n, q_rows, w_a, 0, lambda cols: evec[4, layer:layer + 1, cols])
        project(K, nvis, slice(None), w_a, ed, None)

        def v_rows(j):
            rows = blk(j, 256)
            bias = column_of(evec[5, layer:layer + 1, rows], 128)
            acc = mm_t(w_a[pl.ds(pl.multiple_of(2 * ed + j * 256, 256), 256), :], A[...])
            VT[rows, :] = (acc + jnp.concatenate([bias] * (nvis // 128), axis=1)).astype(BF16)

        loop(ed // 256, v_rows)

        def heads2(p):
            cols = blk(p, 128)
            scores = mm_t(K[:, cols], head_rows(Q[0:rows_n, cols], 2))
            top = jnp.max(scores, axis=0, keepdims=True)
            ex = jnp.exp2((scores - top) * (0.125 * LOG2E))
            prob = (ex * (1.0 / jnp.sum(ex, axis=0, keepdims=True))).astype(BF16)
            ATT[0:rows_n, cols] = unstack_heads(mm(VT[cols, :], prob), 2).astype(BF16)

        loop(ed // 128, heads2)

        def out_cols(j):
            cols = blk(j, 512)
            acc = src[q_rows, cols].astype(F32) + mm(ATT[0:rows_n, :], w_a[3 * ed:4 * ed, cols])
            H1[0:rows_n, cols] = (acc + evec[6, layer:layer + 1, cols]).astype(BF16)

        loop(ed // 512, out_cols)
        wait_down()
        norm_rows(H1, A, rows_n, vec(2), vec(3))

        def up_cols(j):
            half_cols = blk(lax.rem(j, ed // 512), 512)
            acc = mm(A[0:rows_n, :], w_up[:, blk(j, 512)])
            HM[0:rows_n, blk(j, 512)] = gelu(acc + evec[8 + j // (ed // 512), layer:layer + 1, half_cols]).astype(BF16)

        loop(w_up.shape[1] // 512, up_cols)

        def down_cols(j):
            cols = blk(j, 256)
            acc = H1[0:rows_n, cols].astype(F32) + mm(HM[0:rows_n, :], w_down[:, cols])
            H2[0:rows_n, cols] = (acc + evec[7, layer:layer + 1, cols]).astype(BF16)

        loop(ed // 256, down_cols)

    for cp in ld_a:
        cp.wait()
    ld_e = load(w2.at[1], X0, 8)

    def mid0():
        ld_e.start()
        g1[1]()
        for cp in ld_b:
            cp.wait()

    enc_layer(0, X0, Y0, Z0, E, nvis, 0, mid0)
    dh = w_dec.shape[0]
    ld_f = []
    for l in range(2):
        ld_f.append(load(dqkv.at[l], Z0.at[l * d_w:(l + 1) * d_w, 0:dd], 9 + l))
        ld_f.append(load(dwo.at[l], Z0.at[2 * d_w + l * dd:2 * d_w + (l + 1) * dd, 0:dd], 11 + l))
        ld_f.append(load(dw1.at[l], Y0.at[l * dd:(l + 1) * dd, 0:4 * dd], 13 + l))
        ld_f.append(load(dw2.at[l], Z0.at[l * 4 * dd:(l + 1) * 4 * dd, dd:2 * dd], 15 + l))
    ld_f.append(load(w_out, Y0.at[0:dd, 4 * dd:4 * dd + w_out.shape[1]], 17))
    ld_dec = load(w_dec, Y0.at[0:dh, 6 * dd:7 * dd], 18)
    ld_dec.start()
    for cp in ld_f:
        cp.start()
    for cp in ld_c:
        cp.wait()

    def mid1():
        g1[2]()
        ld_d.wait()
        ld_e.wait()

    enc_layer(1, X1, Y1, X0, H2, vis_blk, t * vis_blk, mid1)
    norm_rows(H2, A, vis_blk, efin[0:1, :], efin[1:2, :])
    ld_dec.wait()
    Z[t] = mm(A[0:vis_blk, :], Y0[0:dh, 6 * dd:7 * dd]).astype(BF16)
    stz = []
    for d in range(1, nt):
        stz.append(rcopy(Z.at[t], Z.at[t], s_e.at[56 + d], r_e.at[56 + d], tpeer(d), r))
    for cp in stz:
        cp.start()
    g1[3]()
    for cp in ld_f:
        cp.wait()

    heads_g = 4
    ntok = nt * nr * tok

    def keys_values(layer, a_rows, c):
        rows = blk(c, 256)
        base = layer * d_w
        X1[rows, 0:dd] = mm_t(a_rows, Z0[base + dd:base + 2 * dd, 0:dd]).astype(BF16)
        acc = mm_t(Z0[base + 2 * dd:base + 3 * dd, 0:dd], a_rows)
        bias = column_of(dvec[5, layer:layer + 1, :], 128)
        Y1[0:dd, rows] = (acc + jnp.concatenate([bias] * 2, axis=1)).astype(BF16)

    for d in range(1, nt):
        src = tsrc(d)
        rcopy(Z.at[src], Z.at[src], s_e.at[56 + d], r_e.at[56 + d], t, r).wait_recv()

    per = 256 // tok
    tri_b = tri

    def first_chunk(c):
        tb = c // (nr // per)
        dev0 = lax.rem(c, nr // per) * per
        masks = MB[tb]
        ranks = mm(masks.astype(BF16), tri_b)
        cnt = jnp.sum(masks, axis=1, keepdims=True)
        sub = lax.broadcasted_iota(jnp.int32, (nr, nr), 0)
        lane = lax.broadcasted_iota(jnp.int32, (nr, nr), 1)
        cnt_lane = jnp.sum(jnp.where(sub == lane, cnt, 0.0), axis=0, keepdims=True)
        off = jnp.sum(jnp.where(lane < sub, cnt_lane, 0.0), axis=1, keepdims=True)
        index = jnp.where(masks == 1.0, ranks + off, float(vis_blk))
        cols_t = jnp.concatenate([index, jnp.zeros((128 - nr, 128), F32)], axis=0).T
        pick = lax.broadcasted_iota(jnp.int32, (tok, 128), 1)
        ZT[0:vis_blk, :] = Z[tb]
        ZT[vis_blk:128, :] = jnp.broadcast_to(mtok[...], (128 - vis_blk, dd))
        parts = []
        for q in range(per):
            column = jnp.sum(jnp.where(pick == dev0 + q, cols_t[0:tok, :], 0.0), axis=1, keepdims=True)
            one_hot = jnp.where(column == pick.astype(F32), 1.0, 0.0).astype(BF16)
            u = (mm(one_hot, ZT[...]) + DP[tb, dev0 + q].astype(F32)).astype(BF16)
            X1[pl.ds(pl.multiple_of(c * 256 + q * tok, tok), tok), dd:2 * dd] = u
            parts.append(norm(u, dvec[0, 0:1, :], dvec[1, 0:1, :]))
        HD[...] = jnp.concatenate(parts, axis=0)
        keys_values(0, HD[...], c)

    loop(ntok // 256, first_chunk)

    own = pl.ds(pl.multiple_of((t * nr + r) * tok, tok), tok)
    hidden = X1[own, dd:2 * dd]

    def dec_block(layer, hidden, normed):
        base = layer * d_w
        scale = float(dd // 16) ** -0.5 * LOG2E
        Q[0:tok, 0:dd] = (mm_t(normed, Z0[base:base + dd, 0:dd]) + dvec[4, layer:layer + 1, :]).astype(BF16)

        def group(g):
            cols = blk(g, 128)
            stacked = head_rows(Q[0:tok, cols], heads_g)

            def scores_of(c, top):
                sc = mm_t(X1[blk(c, 256), cols], stacked)
                S[blk(c, 256), :] = sc
                return jnp.maximum(top, jnp.max(sc, axis=0, keepdims=True))

            top = lax.fori_loop(0, ntok // 256, scores_of, jnp.full((1, heads_g * tok), -jnp.inf, F32))

            def probs_of(c, total):
                ex = jnp.exp2((S[blk(c, 256), :] - top) * scale)
                PR[blk(c, 256), :] = ex.astype(BF16)
                return total + jnp.sum(ex, axis=0, keepdims=True)

            total = lax.fori_loop(0, ntok // 256, probs_of, jnp.zeros((1, heads_g * tok), F32))
            out_t = mm(Y1[cols, 0:ntok], PR[...]) * (1.0 / total)
            ATT[0:tok, cols] = unstack_heads(out_t, heads_g).astype(BF16)

        loop(dd // 128, group)
        wo_rows = 2 * d_w + layer * dd
        acc = hidden.astype(F32) + mm(ATT[0:tok, 0:dd], Z0[wo_rows:wo_rows + dd, 0:dd]) + dvec[6, layer:layer + 1, :]
        resid = acc.astype(BF16)
        A[0:tok, 0:dd] = norm(resid, dvec[2, layer:layer + 1, :], dvec[3, layer:layer + 1, :])

        def up_cols(j):
            cols = blk(j, dd)
            up = mm(A[0:tok, 0:dd], Y0[layer * dd:(layer + 1) * dd, cols])
            HM[0:tok, cols] = gelu(up + dvec[8 + j, layer:layer + 1, :]).astype(BF16)

        loop(4, up_cols)
        down = mm(HM[0:tok, 0:4 * dd], Z0[layer * 4 * dd:(layer + 1) * 4 * dd, dd:2 * dd])
        return (resid.astype(F32) + down + dvec[7, layer:layer + 1, :]).astype(BF16)

    hidden = dec_block(0, hidden, norm(hidden, dvec[0, 0:1, :], dvec[1, 0:1, :]))
    A2[t, r] = norm(hidden, dvec[0, 1:2, :], dvec[1, 1:2, :])
    H1[0:tok, 0:dd] = hidden
    g2 = gather(A2, s_h, r_h)
    for step in g2[:4]:
        step()

    def second_chunk(c):
        tb = c // (nr // per)
        dev0 = lax.rem(c, nr // per) * per
        keys_values(1, A2[tb, pl.ds(dev0, per)].reshape(256, dd), c)

    loop(ntok // 256, second_chunk)
    hidden = dec_block(1, H1[0:tok, 0:dd], A2[t, r])
    out[...] = mm(norm(hidden, dfin[0:1, :], dfin[1:2, :]), Y0[0:dd, 4 * dd:4 * dd + w_out.shape[1]])

    for cp in st + fw + st2 + fw2 + stz:
        cp.wait_send()
    g1[4]()
    g2[4]()


def solution(mesh):
    nt, nr = mesh.shape["time"], mesh.shape["region"]

    def local_step(patches, enc_pos, vis_mask, dec_pos, w_embed, b_embed, enc_vec, enc_wqkv, enc_wo, enc_w1, enc_w2, enc_final, w_dec_in, mask_token, dec_vec, dec_wqkv, dec_wo, dec_w1, dec_w2, dec_final, w_out):
        tok = patches.shape[0]
        ed, dd = w_embed.shape[1], w_dec_in.shape[1]
        layers = enc_vec.shape[0]
        nvis = tok * nt * nr // KEEP_DIV
        ntok = tok * nt * nr
        flat = lambda w, width: jnp.transpose(w, (0, 2, 3, 4, 1)).reshape(layers, 3 * width, width)
        small = [patches, enc_pos, vis_mask.reshape(1, tok), dec_pos, b_embed.reshape(1, ed),
                 jnp.transpose(enc_vec, (1, 0, 2)), enc_final, mask_token.reshape(1, dd),
                 jnp.transpose(dec_vec, (1, 0, 2)), dec_final]
        big = [w_embed, flat(enc_wqkv, ed), enc_wo.reshape(layers, ed, ed), enc_w1, enc_w2, w_dec_in,
               flat(dec_wqkv, dd), dec_wo.reshape(layers, dd, dd), dec_w1, dec_w2, w_out]
        scratch = [
            pltpu.VMEM((4 * ed, ed), BF16), pltpu.VMEM((4 * ed, ed), BF16),
            pltpu.VMEM((ed, 4 * ed), BF16), pltpu.VMEM((ed, 4 * ed), BF16), pltpu.VMEM((4 * ed, ed), BF16),
            pltpu.VMEM((nr, tok // 2, ed), BF16), pltpu.VMEM((nr, 8, 128), F32), pltpu.VMEM((nt, nr, 128), F32),
            pltpu.VMEM((nvis, ed), BF16), pltpu.VMEM((nvis, ed), BF16), pltpu.VMEM((nvis, ed), BF16),
            pltpu.VMEM((nvis, ed), BF16), pltpu.VMEM((nvis, ed), BF16), pltpu.VMEM((nvis, ed), BF16),
            pltpu.VMEM((ed, nvis), BF16), pltpu.VMEM((nvis, ed), BF16), pltpu.VMEM((nvis, 4 * ed), BF16),
            pltpu.VMEM((nt, nvis // nt, dd), BF16), pltpu.VMEM((128, dd), BF16),
            pltpu.VMEM((nt, nr, tok, dd), BF16), pltpu.VMEM((nt, nr, tok, dd), BF16),
            pltpu.VMEM((ntok, 4 * tok), F32), pltpu.VMEM((ntok, 4 * tok), BF16), pltpu.VMEM((256, dd), BF16),
            pltpu.SemaphoreType.DMA((24,)),
            pltpu.SemaphoreType.DMA((64,)), pltpu.SemaphoreType.DMA((64,)),
            pltpu.SemaphoreType.DMA((64,)), pltpu.SemaphoreType.DMA((64,)),
            pltpu.SemaphoreType.DMA((64,)), pltpu.SemaphoreType.DMA((64,)),
        ]
        return pl.pallas_call(
            functools.partial(kernel, nt, nr),
            out_shape=jax.ShapeDtypeStruct((tok, w_out.shape[1]), F32),
            in_specs=[pl.BlockSpec(memory_space=pltpu.VMEM)] * len(small) + [pl.BlockSpec(memory_space=pl.ANY)] * len(big),
            out_specs=pl.BlockSpec(memory_space=pltpu.VMEM),
            scratch_shapes=scratch,
            compiler_params=pltpu.CompilerParams(collective_id=0, has_side_effects=True, vmem_limit_bytes=67043328),
            name="mae",
        )(*small, *big)

    token_rows = P(TOKEN_AXES, None)
    token_flags = P(TOKEN_AXES)
    replicated = P()
    in_specs = (token_rows, token_rows, token_flags, token_rows) + (replicated,) * 17
    return jax.shard_map(local_step, mesh=mesh, in_specs=in_specs, out_specs=token_rows, check_vma=False)
```

time: 475 us -> 119 us (0.25)
  waiting for transfers between devices: 159 us -> 0 us
  blocking collectives: 148 us -> 0 us
  Pallas kernels: 0 us -> 116 us
  matrix products: 63.3 us -> 0 us
  local copies, waits for them, and re-layouts: 54.4 us -> 2.88 us
  starting transfers between devices: 16.8 us -> 0 us
  other arithmetic: 15.6 us -> 0 us
  between operations: 15.6 us -> 0.01 us
    all_gather x4 -> x0, waiting for transfers between devices: 154 us -> none  [the longest x2 89.5 us: run_block(): key_rows = gather_rows(qkv_rows[:, 1])]
    all_gather x4 -> x0, blocking collectives: 139 us -> none  [the longest x2 71.1 us: run_block(): value_rows = gather_rows(qkv_rows[:, 2])]
    pallas_call x0 -> x1, Pallas kernels: none -> 116 us  [local_step(): pl.pallas_call(functools.partial(kernel, nt, nr), out_shape=jax.ShapeDtyp...]
    dot_general x19 -> x0, matrix products: 62 us -> none  [the longest x4 23 us: run_block(): jnp.dot(mlp_hidden, w_two, preferred_element_type=jnp.float32)]
    all_gather x4 -> x0, local copies, waits for them, and re-layouts: 37.3 us -> none  [the longest x2 18.7 us: run_block(): key_rows = gather_rows(qkv_rows[:, 1])]
    all_to_all x2 -> x0, starting transfers between devices: 16.3 us -> none  [the longest x1 10.9 us: local_step(): returned = lax.all_to_all(back_rows, 'region', 0, 0, tiled=True)]
    slice x15 -> x0, local copies, waits for them, and re-layouts: 10.9 us -> none  [the longest x2 2.43 us: run_block(): vec_rows[2]]
    sub x6 -> x0, other arithmetic: 8.92 us -> none  [the longest x4 8.81 us: attend(): attn_probs = jax.nn.softmax(scores, axis=-1).astype(jnp.bfloat16)]
  transfers between devices with their start and end apart: 6 -> 0, of which waited for: 5 -> 0; matrix products, arithmetic and copies ran while one was open for 9% -> 0% of each run, Pallas kernels for 0% -> 0%
where the time goes in v1:
time: 119 us
  Pallas kernels  116 us (97%)
  local copies, waits for them, and re-layouts  2.88 us (2%)
    pallas_call x1, Pallas kernels, local_step(): pl.pallas_call(functools.partial(kernel, nt, nr), out_shape=jax.ShapeDtyp...  116 us

profile of v1, /device:TPU:97, one launch (start us, length us, event | category | flops | bytes accessed | tf_op | source)
XLA Modules:
  0.0 119.0 jit_solution(16822769144970417466)
XLA Ops:
  0.0 1.3 %reshape.23.mtok = bf16[1,512]{1,0:T(2,128)(2,1)} reshape(bf16[512]{0:T(512)(128)(2,1)} %param.34) | data formatting | bytes 2048 | tf_op jit(solution)/shard_map/reshape | solution.py:491
  1.3 116.1 %mae.1 = f32[64,768]{1,0:T(8,128)} custom-call(bf16[64,768]{1,0:T(8,128)(2,1)} %patches.1, bf16[64,1024]{1,0:T(8,128)(2,1)} %enc_pos.1, s32[1,64]{1,0:T(1,128)} %bitcast.19, bf16[64,512]{1,0:T(8,128)(2,1)} %dec_pos.1, f32[1,1024]{1,0:T(1,128)} %bitcast.18, f32[12,2,1024]{2,1,0:T(2,128)} %bitcast.16, f32[2,1024]{1,0:T(2,128)} %efin.1, ...), custom_call_target="tpu_custom_call" | custom-call | tf_op jit(solution)/shard_map/mae/pallas_call | solution.py:510
  117.4 1.6 %copy.23 = f32[64,768]{1,0:T(8,128)} copy(f32[64,768]{1,0:T(8,128)} %mae.1) | data formatting | bytes 393216

commit v2 on v1

v2 whole, which is shorter than its diff:
```python
import functools
import jax
import jax.numpy as jnp
from jax import lax
from jax.experimental import pallas as pl
from jax.experimental.pallas import tpu as pltpu
from jax.sharding import PartitionSpec as P

KEEP_DIV = 8
LN_EPS = 1e-6
CORES = 2
TOKEN_AXES = ("batch", "time", "region")
MESH_ID = pl.DeviceIdType.MESH
F32 = jnp.float32
BF16 = jnp.bfloat16
LOG2E = 1.4426950408889634


def mm(lhs, rhs):
    return jnp.dot(lhs, rhs, preferred_element_type=F32)


def mm_t(lhs, rhs):
    return lax.dot_general(lhs, rhs, (((1,), (1,)), ((), ())), preferred_element_type=F32)


def norm(rows, gain, shift):
    rows = rows.astype(F32)
    centered = rows - jnp.mean(rows, axis=-1, keepdims=True)
    variance = jnp.mean(centered * centered, axis=-1, keepdims=True)
    return (centered * lax.rsqrt(variance + LN_EPS) * gain + shift).astype(BF16)


def gelu(val):
    return 0.5 * val * (1.0 + lax.erf(val * 0.7071067811865476))


def loop(count, body):
    lax.fori_loop(0, count, lambda i, c: (body(i), c)[1], 0)


def blk(i, size):
    return pl.ds(pl.multiple_of(i * size, size), size)


def column_of(row, lanes):
    return jnp.broadcast_to(row, (lanes, row.shape[1])).T


def head_rows(q_rows, heads):
    lanes = q_rows.shape[1]
    head = iota(q_rows.shape, 1) // (lanes // heads)
    return jnp.concatenate([jnp.where(head == h, q_rows, jnp.zeros_like(q_rows)) for h in range(heads)], axis=0)


def unstack_heads(out_t, heads):
    out = out_t.T
    rows = out.shape[0] // heads
    head = iota((rows, out.shape[1]), 1) // (out.shape[1] // heads)
    total = jnp.where(head == 0, out[:rows], 0.0)
    for h in range(1, heads):
        total = total + jnp.where(head == h, out[h * rows:(h + 1) * rows], 0.0)
    return total


def rsum(val, axis):
    return jnp.sum(val, axis=axis, keepdims=True)


def rmax(val):
    return jnp.max(val, axis=0, keepdims=True)


def iota(shape, axis):
    return lax.broadcasted_iota(jnp.int32, shape, axis)


def kernel(nt, nr, count, *refs):
    given, refs = refs[:count], refs[count:]
    w_embed, wqkv, wo, w1, w2, w_dec, dqkv, dwo, dw1, dw2, out = refs[:11]
    held, refs = refs[11:11 + count], refs[11 + count:]
    (X0, X1, Y0, Y1, Z0, SS, SL, MT, MB, E, E2, H1, H2, A, Q, K, VT, ATT, HM, Z, IC, DP, A2, HD, QB, OT, ML,
     isem, wsem, s_e, r_e, s_g, r_g, s_h, r_h) = refs
    patches, enc_pos, vis, b_embed, dec_pos, evec, efin, mtok, dvec, dfin = held
    ld_in = [pltpu.make_async_copy(src, dst, isem.at[i]) for i, (src, dst) in enumerate(zip(given, held))]
    for cp in ld_in[2:3] + ld_in[:2]:
        cp.start()
    t = lax.axis_index("time")
    r = lax.axis_index("region")
    nx = nr // CORES
    x, core = r // CORES, lax.rem(r, CORES)
    partner = r + 1 - 2 * core
    tok = patches.shape[0]
    slots = SL.shape[1]
    vis_blk = E.shape[0] // nt
    ed, dd = E.shape[1], dec_pos.shape[1]
    nvis = E.shape[0]

    def xpeer(dx):
        return lax.rem(x + dx, nx) * CORES + core

    def tpeer(dy):
        return lax.rem(t + dy, nt)

    def xsrc(dx):
        return lax.rem(x + nx - dx, nx) * CORES + core

    def tsrc(dy):
        return lax.rem(t + nt - dy, nt)

    def rcopy(src, dst, ssem, rsem, tt, rr):
        return pltpu.make_async_remote_copy(src_ref=src, dst_ref=dst, send_sem=ssem, recv_sem=rsem,
                                            device_id={"time": tt, "region": rr}, device_id_type=MESH_ID)

    def load(src, dst, i):
        return pltpu.make_async_copy(src, dst, wsem.at[i])

    ld_embed = load(w_embed, Y1.at[:w_embed.shape[0], :ed], 0)
    ld_embed.start()
    for cp in ld_in[3:]:
        cp.start()

    barrier = pltpu.get_barrier_semaphore()
    order = [d for d in (1, 3, 2) if d < nx]
    across = [(t, partner, 1 - core)] + [(t, xpeer(d) + f * (1 - 2 * core), core + f * (1 - 2 * core)) for d in order for f in range(CORES)]
    peers = [p[:2] for p in across] + [(tpeer(d), r) for d in range(1, nt)]
    for tt, rr in peers:
        pl.semaphore_signal(barrier, inc=1, device_id={"time": tt, "region": rr}, device_id_type=MESH_ID)

    ld_in[2].wait()
    mask_row = vis[...].astype(F32)
    mask_pad = jnp.concatenate([mask_row, jnp.zeros((1, 128 - tok), F32)], axis=1)
    mask_pad = jnp.broadcast_to(mask_pad, (8, 128))
    MT[r] = mask_pad
    tri = (iota((128, 128), 0) < iota((128, 128), 1)).astype(BF16)
    local_rank = mm(mask_pad.astype(BF16), tri)[:1, :tok]
    selector = jnp.where((local_rank == iota((slots, tok), 0).astype(F32)) & (mask_row == 1.0), 1.0, 0.0).astype(BF16)
    for cp in ld_in[:2] + ld_in[3:]:
        cp.wait()

    ld_embed.wait()
    qkv_w, d_w = 3 * ed, 3 * dd
    ld_a = [load(wqkv.at[0], X0.at[:qkv_w], 1), load(wo.at[0], X0.at[qkv_w:qkv_w + ed], 2)]
    ld_b = [load(w1.at[0], Y0, 3), load(w2.at[0], Z0, 4)]
    ld_c = [load(wqkv.at[1], X1.at[:qkv_w], 5), load(wo.at[1], X1.at[qkv_w:qkv_w + ed], 6)]
    for cp in ld_a + ld_b + ld_c:
        cp.start()

    def embed_cols(j):
        cols = blk(j, 256)
        emb = (mm(patches[...], Y1[:patches.shape[1], cols]) + b_embed[:, cols] + enc_pos[:, cols].astype(F32)).astype(BF16)
        SS[j // 2, :, blk(lax.rem(j, 2), 256)] = mm(selector, emb).astype(BF16)

    loop(ed // 256, embed_cols)
    SL[r] = SS[core]
    ld_d = load(w1.at[1], Y1, 7)
    ld_d.start()
    token_row = jnp.broadcast_to(jnp.concatenate([mtok[i:i + 1, :] for i in range(dd // 128)], axis=1), (128 - vis_blk, dd))
    for tb in range(nt):
        Z[tb, vis_blk:128] = token_row
    pl.semaphore_wait(barrier, len(peers))

    st = []
    for i, (tt, rr, half) in enumerate(across):
        st.append(rcopy(SS.at[half], SL.at[r], s_e.at[i], r_e.at[i], tt, rr))
        st.append(rcopy(MT.at[r], MT.at[r], s_e.at[8 + i], r_e.at[8 + i], tt, rr))
    for cp in st:
        cp.start()
    sources = [partner] + [xsrc(d) + f * (1 - 2 * core) for d in order for f in range(CORES)]
    for i, src in enumerate(sources):
        rcopy(SL.at[src], SL.at[src], s_e.at[i], r_e.at[i], t, partner).wait_recv()
        rcopy(MT.at[src], MT.at[src], s_e.at[8 + i], r_e.at[8 + i], t, partner).wait_recv()

    mask_all = jnp.concatenate([MT[d, :1, :] for d in range(nr)], axis=0)
    MB[t] = mask_all
    counts = rsum(mask_all, 1)
    lane_dev = iota((nr, nr * slots), 1) // slots
    sub_dev = iota((nr, nr * slots), 0)
    lane_cnt = rsum(jnp.where(lane_dev == sub_dev, counts, 0.0), 0)
    lane_off = rsum(jnp.where(sub_dev < lane_dev, counts, 0.0), 0)
    lane_slot = lax.rem(iota((1, nr * slots), 1), slots).astype(F32)
    target = jnp.where(lane_slot < lane_cnt, lane_off + lane_slot, -1.0)
    rank_id = iota((vis_blk, nr * slots), 0).astype(F32)
    compact = jnp.where(target == rank_id, 1.0, 0.0).astype(BF16)
    my_rows = blk(t, vis_blk)

    eh = ed // CORES
    my_cols, other_cols = blk(core, eh), blk(1 - core, eh)
    E[my_rows, my_cols] = mm(compact, SL[...].reshape(nr * slots, eh)).astype(BF16)

    mine = E.at[my_rows, my_cols]
    st2 = []
    for d in range(1, nt):
        st2.append(rcopy(mine, mine, s_e.at[32 + d], r_e.at[32 + d], tpeer(d), r))
        st2.append(rcopy(MB.at[t], MB.at[t], s_e.at[40 + d], r_e.at[40 + d], tpeer(d), r))
    st2.append(rcopy(mine, mine, s_e.at[48], r_e.at[48], t, partner))
    for cp in st2:
        cp.start()
    DP[t, r] = dec_pos[...]

    def gather(buf, ss, rs):
        hw = dd // 2
        first, second, third = [], [], {}

        def step1():
            own = buf.at[t, r]
            for d in order:
                first.append(rcopy(own, own, ss.at[d], rs.at[d], tpeer(d), r))
                first.append(rcopy(own, own, ss.at[4 + d], rs.at[4 + d], t, xpeer(d)))
            first.append(rcopy(own, own, ss.at[0], rs.at[0], t, partner))
            for cp in first:
                cp.start()

        def to_partner(ref, d, e):
            i = 40 + d * 4 + e
            cp = rcopy(ref, ref, ss.at[i], rs.at[i], t, partner)
            cp.start()
            third[(d, e)] = cp

        def step2(d):
            src = tsrc(d)
            rcopy(buf.at[src, r], buf.at[src, r], ss.at[d], rs.at[d], t, partner).wait_recv()
            for e in range(1, nx):
                i = 8 + d * 4 + e
                low = buf.at[src, r, :, :hw]
                second.append(rcopy(low, low, ss.at[i], rs.at[i], t, xpeer(e)))
                second[-1].start()
            to_partner(buf.at[src, r], d, 0)
            src = xsrc(d)
            rcopy(buf.at[t, src], buf.at[t, src], ss.at[4 + d], rs.at[4 + d], t, partner).wait_recv()
            for e in range(1, nt):
                i = 24 + d * 4 + e
                high = buf.at[t, src, :, hw:]
                second.append(rcopy(high, high, ss.at[i], rs.at[i], tpeer(e), r))
                second[-1].start()
            to_partner(buf.at[t, src], 0, d)

        def step3(d, e):
            ref = buf.at[tsrc(d), xsrc(e)]
            low, high = ref.at[:, :hw], ref.at[:, hw:]
            rcopy(low, low, ss.at[8 + d * 4 + e], rs.at[8 + d * 4 + e], t, partner).wait_recv()
            rcopy(high, high, ss.at[24 + e * 4 + d], rs.at[24 + e * 4 + d], t, partner).wait_recv()
            to_partner(ref, d, e)

        def finish(d, e):
            if d == 0 and e == 0:
                rcopy(buf.at[t, partner], buf.at[t, partner], ss.at[0], rs.at[0], t, partner).wait_recv()
            else:
                third[(d, e)].wait_recv()

        def drain():
            for cp in first + second + list(third.values()):
                cp.wait_send()

        return step1, step2, step3, finish, drain

    g1 = gather(DP, s_g, r_g)
    g1[0]()

    def index_cols(masks):
        ranks = mm(masks.astype(BF16), tri)
        sub, lane = iota((nr, nr), 0), iota((nr, nr), 1)
        cnt_lane = rsum(jnp.where(sub == lane, rsum(masks, 1), 0.0), 0)
        off = rsum(jnp.where(lane < sub, cnt_lane, 0.0), 1)
        index = jnp.where(masks == 1.0, ranks + off, float(vis_blk))
        return jnp.concatenate([index, jnp.zeros((128 - nr, 128), F32)], axis=0).T

    def norm_rows(src, dst, count, gain, shift, start, dst_start, step=64):
        def body(i):
            rows = pl.ds(pl.multiple_of(start + i * step, step), step)
            dst[pl.ds(pl.multiple_of(dst_start + i * step, step), step), :] = norm(src[rows, :], gain, shift)
        loop(count // step, body)

    fw2 = []

    def rows0(vec):
        def take(block, i):
            got = E.at[blk(block, vis_blk), other_cols]
            rcopy(got, got, s_e.at[48 + i], r_e.at[48 + i], t, partner).wait_recv()
            norm_rows(E, A, vis_blk, vec(0), vec(1), block * vis_blk, block * vis_blk)

        take(t, 0)
        for d in order:
            got = E.at[blk(tsrc(d), vis_blk), my_cols]
            rcopy(got, got, s_e.at[32 + d], r_e.at[32 + d], t, partner).wait_recv()
            fw2.append(rcopy(got, got, s_e.at[48 + d], r_e.at[48 + d], t, partner))
            fw2[-1].start()
            rcopy(MB.at[tsrc(d)], MB.at[tsrc(d)], s_e.at[40 + d], r_e.at[40 + d], t, partner).wait_recv()
        for d in order:
            take(tsrc(d), d)

    def project(dst, rows_n, src_rows, w, w_row, bias):
        def body(j):
            cols = blk(j, 512)
            acc = mm_t(A[src_rows, :], w[pl.ds(pl.multiple_of(w_row + j * 512, 512), 512), :])
            if bias is not None:
                acc = acc + bias(cols)
            dst[:rows_n, cols] = acc.astype(BF16)
        loop(ed // 512, body)

    def enc_layer(layer, w_a, w_up, w_down, src, dst, rows_n, start, dst_start, pairs, wait_rows, wait_down):
        def vec(i):
            return evec[i, layer:layer + 1, :]

        wait_rows(vec)
        q_rows = pl.ds(pl.multiple_of(start, rows_n), rows_n)
        project(Q, rows_n, q_rows, w_a, 0, lambda cols: evec[4, layer:layer + 1, cols])
        project(K, nvis, slice(None), w_a, ed, None)

        def v_rows(j):
            rows = blk(j, 512)
            bias = column_of(evec[5, layer:layer + 1, rows], 128)
            acc = mm_t(w_a[pl.ds(pl.multiple_of(2 * ed + j * 512, 512), 512), :], A[...])
            VT[rows, :] = (acc + jnp.concatenate([bias] * (nvis // 128), axis=1)).astype(BF16)

        loop(ed // 512, v_rows)

        def heads2(p):
            for q in range(pairs):
                cols = blk(p * pairs + q, 128)
                scores = mm_t(K[:, cols], head_rows(Q[:rows_n, cols], 2))
                top = rmax(scores)
                ex = jnp.exp2((scores - top) * (0.125 * LOG2E))
                prob = (ex * (1.0 / rsum(ex, 0))).astype(BF16)
                ATT[:rows_n, cols] = unstack_heads(mm(VT[cols, :], prob), 2).astype(BF16)

        loop(ed // 128 // pairs, heads2)

        def out_cols(j):
            cols = blk(j, 512)
            acc = src[q_rows, cols].astype(F32) + mm(ATT[:rows_n, :], w_a[3 * ed:4 * ed, cols])
            H1[:rows_n, cols] = (acc + evec[6, layer:layer + 1, cols]).astype(BF16)

        loop(ed // 512, out_cols)
        wait_down()
        norm_rows(H1, A, rows_n, vec(2), vec(3), 0, 0)

        def up_cols(j):
            acc = mm(A[:rows_n, :], w_up[:, blk(j, ed)])
            HM[:rows_n, blk(j, ed)] = gelu(acc + evec[8 + j, layer:layer + 1, :]).astype(BF16)

        loop(w_up.shape[1] // ed, up_cols)
        o_rows = pl.ds(pl.multiple_of(dst_start, rows_n), rows_n)

        def down_cols(j):
            cols = blk(j, 256)
            acc = H1[:rows_n, cols].astype(F32) + mm(HM[:rows_n, :], w_down[:, cols])
            dst[o_rows, cols] = (acc + evec[7, layer:layer + 1, cols]).astype(BF16)

        loop(ed // 256, down_cols)

    for cp in ld_a:
        cp.wait()
    ld_e = load(w2.at[1], X0, 8)

    def mid0():
        ld_e.start()
        for d in order:
            g1[1](d)
        for cp in ld_b:
            cp.wait()

    hv = nvis // CORES
    enc_layer(0, X0, Y0, Z0, E, H2, hv, core * hv, core * hv, 2,
              rows0, mid0)
    h_mine = pl.ds(pl.multiple_of(core * hv, hv), hv)
    swap = rcopy(H2.at[h_mine], H2.at[h_mine], s_e.at[60], r_e.at[60], t, partner)
    swap.start()
    dh = w_dec.shape[0]
    ld_f = []
    for l in range(2):
        ld_f.append(load(dqkv.at[l], Z0.at[l * d_w:(l + 1) * d_w, :dd], 9 + l))
        ld_f.append(load(dwo.at[l], Z0.at[2 * d_w + l * dd:2 * d_w + (l + 1) * dd, :dd], 11 + l))
        ld_f.append(load(dw1.at[l], Y0.at[l * dd:(l + 1) * dd, :4 * dd], 13 + l))
        ld_f.append(load(dw2.at[l], Z0.at[l * 4 * dd:(l + 1) * 4 * dd, dd:2 * dd], 15 + l))
    ld_dec = load(w_dec, Y0.at[:dh, 6 * dd:7 * dd], 18)
    ld_dec.start()
    for cp in ld_f:
        cp.start()
    for cp in ld_c:
        cp.wait()

    def mid1():
        for d in order:
            for e in order:
                g1[2](d, e)
        ld_d.wait()
        ld_e.wait()

    def rows1(vec):
        norm_rows(H2, A, hv, vec(0), vec(1), core * hv, core * hv)
        other = pl.ds(pl.multiple_of((1 - core) * hv, hv), hv)
        rcopy(H2.at[other], H2.at[other], s_e.at[60], r_e.at[60], t, partner).wait_recv()
        norm_rows(H2, A, hv, vec(0), vec(1), (1 - core) * hv, (1 - core) * hv)

    enc_layer(1, X1, Y1, X0, H2, E2, vis_blk, t * vis_blk, 0, 4, rows1, mid1)
    norm_rows(E2, A, vis_blk, efin[:1, :], efin[1:2, :], 0, 0)
    ld_dec.wait()
    z_mine = Z.at[t, :vis_blk]
    Z[t, :vis_blk] = mm(A[:vis_blk, :], Y0[:dh, 6 * dd:7 * dd]).astype(BF16)
    stz = []
    for d in range(1, nt):
        stz.append(rcopy(z_mine, z_mine, s_e.at[56 + d], r_e.at[56 + d], tpeer(d), r))
    for cp in stz:
        cp.start()
    for tb in range(nt):
        IC[tb] = index_cols(MB[tb])
    for d in range(nt):
        for e in range(nx):
            g1[3](d, e)
    for cp in ld_f:
        cp.wait()

    groups = dd // 128
    heads_g = 4
    stack = heads_g * tok
    scale = float(dd // (groups * heads_g)) ** -0.5 * LOG2E
    blk_tok = nr * tok

    pick = iota((tok, 128), 1)

    def one_hot(column):
        return jnp.where(column == pick.astype(F32), 1.0, 0.0).astype(BF16)

    own_col = rsum(jnp.where(pick == r, IC[t, :tok, :], 0.0), 1)
    hidden = (mm(one_hot(own_col), Z[t]) + DP[t, r].astype(F32)).astype(BF16)

    def start_attention(layer, normed):
        base = layer * d_w
        q_all = (mm_t(normed, Z0[base:base + dd, :dd]) + dvec[4, layer:layer + 1, :]).astype(BF16)
        for g in range(groups):
            QB[g] = head_rows(q_all[:, g * 128:(g + 1) * 128], heads_g)
        OT[...] = jnp.zeros(OT.shape, F32)
        ML[:groups] = jnp.full((groups, 1, stack), -jnp.inf, F32)
        ML[groups:2 * groups] = jnp.zeros((groups, 1, stack), F32)

    def attend(layer, rows):
        base = layer * d_w
        keys = mm_t(rows, Z0[base + dd:base + 2 * dd, :dd]).astype(BF16)
        acc = mm_t(Z0[base + 2 * dd:base + 3 * dd, :dd], rows)
        bias = column_of(dvec[5, layer:layer + 1, :], 128)
        values = (acc + jnp.concatenate([bias] * (rows.shape[0] // 128), axis=1)).astype(BF16)
        for g in range(groups):
            sc = mm_t(keys[:, g * 128:(g + 1) * 128], QB[g])
            old = ML[g]
            top = jnp.maximum(old, rmax(sc))
            ex = jnp.exp2((sc - top) * scale)
            keep = jnp.exp2((old - top) * scale)
            ML[g] = top
            ML[groups + g] = ML[groups + g] * keep + rsum(ex, 0)
            lanes = slice(g * 128, (g + 1) * 128)
            OT[lanes, :] = OT[lanes, :] * keep + mm(values[lanes, :], ex.astype(BF16))

    def finish_block(layer, hidden):
        for g in range(groups):
            lanes = slice(g * 128, (g + 1) * 128)
            ATT[:tok, lanes] = unstack_heads(OT[lanes, :] * (1.0 / ML[groups + g]), heads_g).astype(BF16)
        wo_rows = 2 * d_w + layer * dd
        acc = hidden.astype(F32) + mm(ATT[:tok, :dd], Z0[wo_rows:wo_rows + dd, :dd]) + dvec[6, layer:layer + 1, :]
        resid = acc.astype(BF16)
        normed = norm(resid, dvec[2, layer:layer + 1, :], dvec[3, layer:layer + 1, :])
        for j in range(4):
            cols = slice(j * dd, (j + 1) * dd)
            up = mm(normed, Y0[layer * dd:(layer + 1) * dd, cols])
            HM[:tok, cols] = gelu(up + dvec[8 + j, layer:layer + 1, :]).astype(BF16)
        down = mm(HM[:tok, :4 * dd], Z0[layer * 4 * dd:(layer + 1) * 4 * dd, dd:2 * dd])
        return (resid.astype(F32) + down + dvec[7, layer:layer + 1, :]).astype(BF16)

    start_attention(0, norm(hidden, dvec[0, :1, :], dvec[1, :1, :]))

    def first_unit(d):
        tb = lax.rem(t + nt - d, nt)
        cols_t = IC[tb]

        @pl.when(d > 0)
        def _():
            ref = Z.at[tb, :vis_blk]
            rcopy(ref, ref, s_e.at[56 + d], r_e.at[56 + d], t, r).wait_recv()

        for q in range(nr):
            u = (mm(one_hot(cols_t[:tok, q:q + 1]), Z[tb]) + DP[tb, q].astype(F32)).astype(BF16)
            HD[q * tok:(q + 1) * tok, :] = norm(u, dvec[0, :1, :], dvec[1, :1, :])
        attend(0, HD[...])

    loop(nt, first_unit)
    hidden = finish_block(0, hidden)
    A2[t, r] = norm(hidden, dvec[0, 1:2, :], dvec[1, 1:2, :])
    H1[:tok, :dd] = hidden
    g2 = gather(A2, s_h, r_h)
    g2[0]()
    start_attention(1, A2[t, r])

    def unit(*chips):
        parts = []
        for d, e in chips:
            g2[3](d, e)
            xs = lax.rem(x + nx - e, nx) * CORES
            parts.append(A2[tsrc(d), pl.ds(xs, CORES)].reshape(CORES * tok, dd))
        attend(1, jnp.concatenate(parts, axis=0))

    g2[1](1)
    g2[1](3)
    unit((0, 0), (1, 0), (3, 0), (0, 1))
    g2[1](2)
    unit((0, 3), (2, 0), (0, 2))
    near = [(1, 1), (1, 3), (3, 1), (3, 3)]
    far = [(1, 2), (2, 1), (2, 3), (3, 2)]
    for d, e in near + far:
        g2[2](d, e)
    unit(*near)
    g2[2](2, 2)
    unit(*far, (2, 2))
    hidden = finish_block(1, H1[:tok, :dd])
    out[...] = norm(hidden, dfin[:1, :], dfin[1:2, :])

    for cp in st + st2 + fw2 + stz + [swap]:
        cp.wait_send()
    g1[4]()
    g2[4]()


def solution(mesh):
    nt, nr = mesh.shape["time"], mesh.shape["region"]

    def local_step(patches, enc_pos, vis_mask, dec_pos, w_embed, b_embed, enc_vec, enc_wqkv, enc_wo, enc_w1, enc_w2, enc_final, w_dec_in, mask_token, dec_vec, dec_wqkv, dec_wo, dec_w1, dec_w2, dec_final, w_out):
        tok = patches.shape[0]
        ed, dd = w_embed.shape[1], w_dec_in.shape[1]
        layers = enc_vec.shape[0]
        nvis = tok * nt * nr // KEEP_DIV
        flat = lambda w, width: jnp.transpose(w, (0, 2, 3, 4, 1)).reshape(layers, 3 * width, width)
        small = [patches, enc_pos, vis_mask.reshape(1, tok), b_embed.reshape(1, ed), dec_pos,
                 jnp.transpose(enc_vec, (1, 0, 2)), enc_final, mask_token.reshape(dd // 128, 128),
                 jnp.transpose(dec_vec, (1, 0, 2)), dec_final]
        big = [w_embed, flat(enc_wqkv, ed), enc_wo.reshape(layers, ed, ed), enc_w1, enc_w2, w_dec_in,
               flat(dec_wqkv, dd), dec_wo.reshape(layers, dd, dd), dec_w1, dec_w2]
        scratch = [pltpu.VMEM(v.shape, v.dtype) for v in small] + [
            pltpu.VMEM((4 * ed, ed), BF16), pltpu.VMEM((4 * ed, ed), BF16),
            pltpu.VMEM((ed, 4 * ed), BF16), pltpu.VMEM((ed, 4 * ed), BF16), pltpu.VMEM((4 * ed, ed), BF16),
            pltpu.VMEM((CORES, tok // 2, ed // CORES), BF16), pltpu.VMEM((nr, tok // 2, ed // CORES), BF16), pltpu.VMEM((nr, 8, 128), F32), pltpu.VMEM((nt, nr, 128), F32),
            pltpu.VMEM((nvis, ed), BF16), pltpu.VMEM((nvis // nt, ed), BF16), pltpu.VMEM((nvis // CORES, ed), BF16), pltpu.VMEM((nvis, ed), BF16),
            pltpu.VMEM((nvis, ed), BF16), pltpu.VMEM((nvis // CORES, ed), BF16), pltpu.VMEM((nvis, ed), BF16),
            pltpu.VMEM((ed, nvis), BF16), pltpu.VMEM((nvis // CORES, ed), BF16), pltpu.VMEM((nvis // CORES, 4 * ed), BF16),
            pltpu.VMEM((nt, 128, dd), BF16), pltpu.VMEM((nt, 128, 128), F32),
            pltpu.VMEM((nt, nr, tok, dd), BF16), pltpu.VMEM((nt, nr, tok, dd), BF16),
            pltpu.VMEM((nr * tok, dd), BF16), pltpu.VMEM((dd // 128, 4 * tok, 128), BF16),
            pltpu.VMEM((dd, 4 * tok), F32), pltpu.VMEM((2 * dd // 128, 1, 4 * tok), F32),
        ] + [pltpu.SemaphoreType.DMA((n,)) for n in (16, 24) + (64,) * 6]
        rows = pl.pallas_call(
            functools.partial(kernel, nt, nr, len(small)),
            out_shape=jax.ShapeDtypeStruct((tok, dd), BF16),
            in_specs=[pl.BlockSpec(memory_space=pl.ANY)] * (len(small) + len(big)),
            out_specs=pl.BlockSpec(memory_space=pltpu.VMEM),
            scratch_shapes=scratch,
            compiler_params=pltpu.CompilerParams(collective_id=0, has_side_effects=True, vmem_limit_bytes=64 * 1024 * 1024 - 65536),
            name="mae",
        )(*small, *big)
        return mm(rows, w_out)

    token_rows = P(TOKEN_AXES, None)
    token_flags = P(TOKEN_AXES)
    replicated = P()
    in_specs = (token_rows, token_rows, token_flags, token_rows) + (replicated,) * 17
    return jax.shard_map(local_step, mesh=mesh, in_specs=in_specs, out_specs=token_rows, check_vma=False)
```

time: 119 us -> 86.5 us (0.73)
  Pallas kernels: 116 us -> 84.2 us
  local copies, waits for them, and re-layouts: 2.88 us -> 0 us
  matrix products: 0 us -> 2.11 us
    pallas_call x1, Pallas kernels: 116 us -> 84.2 us  [local_step(): pl.pallas_call(functools.partial(kernel, nt, nr, len(small)), out_shape=j...]
    dot_general x0 -> x1, matrix products: none -> 2.11 us  [mm(): return jnp.dot(lhs, rhs, preferred_element_type=F32)]
    unnamed x1 -> x0, local copies, waits for them, and re-layouts: 1.62 us -> none
    reshape x1 -> x0, local copies, waits for them, and re-layouts: 1.26 us -> none  [local_step(): mask_token.reshape(1, dd)]
where the time goes in v2:
time: 86.5 us; the launch traced here: 86.3 us
  Pallas kernels  84.2 us (97%)
  matrix products  2.11 us (2%)
    pallas_call x1, Pallas kernels, local_step(): pl.pallas_call(functools.partial(kernel, nt, nr, len(small)), out_shape=j...  84.2 us
    dot_general x1, matrix products, mm(): return jnp.dot(lhs, rhs, preferred_element_type=F32)  2.11 us

profile of v2, /device:TPU:97, one launch (start us, length us, event | category | flops | bytes accessed | tf_op | source)
XLA Modules:
  0.0 86.3 jit_solution(7426095077718898298)
XLA Ops:
  0.0 84.2 %mae.1 = bf16[64,512]{1,0:T(8,128)(2,1)} custom-call(bf16[64,768]{1,0:T(8,128)(2,1)} %refs_0_.1, bf16[64,1024]{1,0:T(8,128)(2,1)} %refs_1_.1, s32[1,64]{1,0:T(1,128)} %bitcast.23, f32[1,1024]{1,0:T(1,128)} %bitcast.21, bf16[64,512]{1,0:T(8,128)(2,1)} %refs_4_.1, f32[12,2,1024]{2,1,0:T(2,128)} %bitcast.19, f32[2,1024]{1,0:T(2,128)} %refs_6_.1, ...), custom_call_target="tpu_custom_call" | custom-call | tf_op jit(solution)/shard_map/mae/pallas_call | solution.py:548
  84.2 2.1 %fusion = f32[64,768]{1,0:T(8,128)} fusion(bf16[64,512]{1,0:T(8,128)(2,1)} %mae.1, bf16[512,768]{1,0:T(8,128)(2,1)} %param.41), kind=kOutput, calls=%fused_computation | convolution fusion | flops 50331648 | bytes 1048576 | tf_op jit(solution)/shard_map/dot_general | solution.py:20

commit v3 on v2

--- a/solution.py
+++ b/solution.py
@@ -361,7 +361,7 @@
             cp.wait()
 
     hv = nvis // CORES
-    enc_layer(0, X0, Y0, Z0, E, H2, hv, core * hv, core * hv, 2,
+    enc_layer(0, X0, Y0, Z0, E, H2, hv, core * hv, core * hv, 8,
               rows0, mid0)
     h_mine = pl.ds(pl.multiple_of(core * hv, hv), hv)
     swap = rcopy(H2.at[h_mine], H2.at[h_mine], s_e.at[60], r_e.at[60], t, partner)
@@ -393,7 +393,7 @@
         rcopy(H2.at[other], H2.at[other], s_e.at[60], r_e.at[60], t, partner).wait_recv()
         norm_rows(H2, A, hv, vec(0), vec(1), (1 - core) * hv, (1 - core) * hv)
 
-    enc_layer(1, X1, Y1, X0, H2, E2, vis_blk, t * vis_blk, 0, 4, rows1, mid1)
+    enc_layer(1, X1, Y1, X0, H2, E2, vis_blk, t * vis_blk, 0, 8, rows1, mid1)
     norm_rows(E2, A, vis_blk, efin[:1, :], efin[1:2, :], 0, 0)
     ld_dec.wait()
     z_mine = Z.at[t, :vis_blk]
@@ -468,21 +468,21 @@
 
     start_attention(0, norm(hidden, dvec[0, :1, :], dvec[1, :1, :]))
 
-    def first_unit(d):
-        tb = lax.rem(t + nt - d, nt)
+    def first_rows(d):
+        tb = tsrc(d)
+        if d > 0:
+            ref = Z.at[tb, :vis_blk]
+            rcopy(ref, ref, s_e.at[56 + d], r_e.at[56 + d], t, partner).wait_recv()
         cols_t = IC[tb]
-
-        @pl.when(d > 0)
-        def _():
-            ref = Z.at[tb, :vis_blk]
-            rcopy(ref, ref, s_e.at[56 + d], r_e.at[56 + d], t, r).wait_recv()
-
         for q in range(nr):
             u = (mm(one_hot(cols_t[:tok, q:q + 1]), Z[tb]) + DP[tb, q].astype(F32)).astype(BF16)
-            HD[q * tok:(q + 1) * tok, :] = norm(u, dvec[0, :1, :], dvec[1, :1, :])
-        attend(0, HD[...])
-
-    loop(nt, first_unit)
+            HD[d, q * tok:(q + 1) * tok, :] = norm(u, dvec[0, :1, :], dvec[1, :1, :])
+
+    first_rows(0)
+    for d in range(1, nt):
+        first_rows(d)
+        attend(0, HD[d - 1])
+    attend(0, HD[nt - 1])
     hidden = finish_block(0, hidden)
     A2[t, r] = norm(hidden, dvec[0, 1:2, :], dvec[1, 1:2, :])
     H1[:tok, :dd] = hidden
@@ -498,18 +498,16 @@
             parts.append(A2[tsrc(d), pl.ds(xs, CORES)].reshape(CORES * tok, dd))
         attend(1, jnp.concatenate(parts, axis=0))
 
-    g2[1](1)
-    g2[1](3)
+    for d in order:
+        g2[1](d)
     unit((0, 0), (1, 0), (3, 0), (0, 1))
-    g2[1](2)
     unit((0, 3), (2, 0), (0, 2))
     near = [(1, 1), (1, 3), (3, 1), (3, 3)]
-    far = [(1, 2), (2, 1), (2, 3), (3, 2)]
+    far = [(1, 2), (2, 1), (2, 3), (3, 2), (2, 2)]
     for d, e in near + far:
         g2[2](d, e)
     unit(*near)
-    g2[2](2, 2)
-    unit(*far, (2, 2))
+    unit(*far)
     hidden = finish_block(1, H1[:tok, :dd])
     out[...] = norm(hidden, dfin[:1, :], dfin[1:2, :])
 
@@ -542,7 +540,7 @@
             pltpu.VMEM((ed, nvis), BF16), pltpu.VMEM((nvis // CORES, ed), BF16), pltpu.VMEM((nvis // CORES, 4 * ed), BF16),
             pltpu.VMEM((nt, 128, dd), BF16), pltpu.VMEM((nt, 128, 128), F32),
             pltpu.VMEM((nt, nr, tok, dd), BF16), pltpu.VMEM((nt, nr, tok, dd), BF16),
-            pltpu.VMEM((nr * tok, dd), BF16), pltpu.VMEM((dd // 128, 4 * tok, 128), BF16),
+            pltpu.VMEM((nt, nr * tok, dd), BF16), pltpu.VMEM((dd // 128, 4 * tok, 128), BF16),
             pltpu.VMEM((dd, 4 * tok), F32), pltpu.VMEM((2 * dd // 128, 1, 4 * tok), F32),
         ] + [pltpu.SemaphoreType.DMA((n,)) for n in (16, 24) + (64,) * 6]
         rows = pl.pallas_call(

time: 86.5 us -> 83.7 us (0.968)
  Pallas kernels: 84.2 us -> 81.5 us
    pallas_call x1, Pallas kernels: 84.2 us -> 81.5 us  [local_step(): pl.pallas_call(functools.partial(kernel, nt, nr, len(small)), out_shape=j...]
where the time goes in v3:
time: 83.7 us; the launch traced here: 83.6 us
  Pallas kernels  81.5 us (97%)
  matrix products  2.11 us (3%)
    pallas_call x1, Pallas kernels, local_step(): pl.pallas_call(functools.partial(kernel, nt, nr, len(small)), out_shape=j...  81.5 us
    dot_general x1, matrix products, mm(): return jnp.dot(lhs, rhs, preferred_element_type=F32)  2.11 us

profile of v3, /device:TPU:97, one launch (start us, length us, event | category | flops | bytes accessed | tf_op | source)
XLA Modules:
  0.0 83.6 jit_solution(5047952769835832913)
XLA Ops:
  0.0 81.5 %mae.1 = bf16[64,512]{1,0:T(8,128)(2,1)} custom-call(bf16[64,768]{1,0:T(8,128)(2,1)} %refs_0_.1, bf16[64,1024]{1,0:T(8,128)(2,1)} %refs_1_.1, s32[1,64]{1,0:T(1,128)} %bitcast.23, f32[1,1024]{1,0:T(1,128)} %bitcast.21, bf16[64,512]{1,0:T(8,128)(2,1)} %refs_4_.1, f32[12,2,1024]{2,1,0:T(2,128)} %bitcast.19, f32[2,1024]{1,0:T(2,128)} %refs_6_.1, ...), custom_call_target="tpu_custom_call" | custom-call | tf_op jit(solution)/shard_map/mae/pallas_call | solution.py:546
  81.5 2.1 %fusion = f32[64,768]{1,0:T(8,128)} fusion(bf16[64,512]{1,0:T(8,128)(2,1)} %mae.1, bf16[512,768]{1,0:T(8,128)(2,1)} %param.41), kind=kOutput, calls=%fused_computation | convolution fusion | flops 50331648 | bytes 1048576 | tf_op jit(solution)/shard_map/dot_general | solution.py:20

commit v4 on v3

--- a/solution.py
+++ b/solution.py
@@ -91,7 +91,7 @@
     x, core = r // CORES, lax.rem(r, CORES)
     partner = r + 1 - 2 * core
     tok = patches.shape[0]
-    slots = SL.shape[1]
+    slots = SL.shape[2]
     vis_blk = E.shape[0] // nt
     ed, dd = E.shape[1], dec_pos.shape[1]
     nvis = E.shape[0]
@@ -115,8 +115,14 @@
     def load(src, dst, i):
         return pltpu.make_async_copy(src, dst, wsem.at[i])
 
-    ld_embed = load(w_embed, Y1.at[:w_embed.shape[0], :ed], 0)
-    ld_embed.start()
+    quarter = ed // 4
+    subs = range(2)
+    chunks = [half * 2 + sub for sub in subs for half in range(CORES)]
+    ld_embed = {}
+    for j in chunks:
+        cols = slice(j * quarter, (j + 1) * quarter)
+        ld_embed[j] = load(w_embed.at[:, cols], Y1.at[:w_embed.shape[0], cols], 20 + j)
+        ld_embed[j].start()
     for cp in ld_in[3:]:
         cp.start()
 
@@ -138,37 +144,45 @@
     for cp in ld_in[:2] + ld_in[3:]:
         cp.wait()
 
-    ld_embed.wait()
     qkv_w, d_w = 3 * ed, 3 * dd
     ld_a = [load(wqkv.at[0], X0.at[:qkv_w], 1), load(wo.at[0], X0.at[qkv_w:qkv_w + ed], 2)]
     ld_b = [load(w1.at[0], Y0, 3), load(w2.at[0], Z0, 4)]
     ld_c = [load(wqkv.at[1], X1.at[:qkv_w], 5), load(wo.at[1], X1.at[qkv_w:qkv_w + ed], 6)]
-    for cp in ld_a + ld_b + ld_c:
+    def embed_chunk(j):
+        ld_embed[j].wait()
+        cols = slice(j * quarter, (j + 1) * quarter)
+        emb = (mm(patches[...], Y1[:patches.shape[1], cols]) + b_embed[:, cols] + enc_pos[:, cols].astype(F32)).astype(BF16)
+        SS[j] = mm(selector, emb).astype(BF16)
+
+    st = []
+    for sub in subs:
+        for half in range(CORES):
+            embed_chunk(half * 2 + sub)
+        SL[sub, r] = SS[core * 2 + sub]
+        if sub == 0:
+            pl.semaphore_wait(barrier, len(peers))
+        for i, (tt, rr, half) in enumerate(across):
+            st.append(rcopy(SS.at[half * 2 + sub], SL.at[sub, r], s_e.at[16 * sub + i], r_e.at[16 * sub + i], tt, rr))
+            st[-1].start()
+            if sub == 0:
+                st.append(rcopy(MT.at[r], MT.at[r], s_e.at[8 + i], r_e.at[8 + i], tt, rr))
+                st[-1].start()
+    ld_d = load(w1.at[1], Y1, 7)
+    for cp in ld_a + ld_b + ld_c + [ld_d]:
         cp.start()
-
-    def embed_cols(j):
-        cols = blk(j, 256)
-        emb = (mm(patches[...], Y1[:patches.shape[1], cols]) + b_embed[:, cols] + enc_pos[:, cols].astype(F32)).astype(BF16)
-        SS[j // 2, :, blk(lax.rem(j, 2), 256)] = mm(selector, emb).astype(BF16)
-
-    loop(ed // 256, embed_cols)
-    SL[r] = SS[core]
-    ld_d = load(w1.at[1], Y1, 7)
-    ld_d.start()
     token_row = jnp.broadcast_to(jnp.concatenate([mtok[i:i + 1, :] for i in range(dd // 128)], axis=1), (128 - vis_blk, dd))
     for tb in range(nt):
         Z[tb, vis_blk:128] = token_row
-    pl.semaphore_wait(barrier, len(peers))
-
-    st = []
-    for i, (tt, rr, half) in enumerate(across):
-        st.append(rcopy(SS.at[half], SL.at[r], s_e.at[i], r_e.at[i], tt, rr))
-        st.append(rcopy(MT.at[r], MT.at[r], s_e.at[8 + i], r_e.at[8 + i], tt, rr))
-    for cp in st:
-        cp.start()
+    DP[t, r] = dec_pos[...]
     sources = [partner] + [xsrc(d) + f * (1 - 2 * core) for d in order for f in range(CORES)]
+
+    def slots_arrive(sub):
+        for i, src in enumerate(sources):
+            got = SL.at[sub, src]
+            rcopy(got, got, s_e.at[16 * sub + i], r_e.at[16 * sub + i], t, partner).wait_recv()
+
+    slots_arrive(0)
     for i, src in enumerate(sources):
-        rcopy(SL.at[src], SL.at[src], s_e.at[i], r_e.at[i], t, partner).wait_recv()
         rcopy(MT.at[src], MT.at[src], s_e.at[8 + i], r_e.at[8 + i], t, partner).wait_recv()
 
     mask_all = jnp.concatenate([MT[d, :1, :] for d in range(nr)], axis=0)
@@ -184,19 +198,23 @@
     compact = jnp.where(target == rank_id, 1.0, 0.0).astype(BF16)
     my_rows = blk(t, vis_blk)
 
-    eh = ed // CORES
-    my_cols, other_cols = blk(core, eh), blk(1 - core, eh)
-    E[my_rows, my_cols] = mm(compact, SL[...].reshape(nr * slots, eh)).astype(BF16)
-
-    mine = E.at[my_rows, my_cols]
+
+    def part(which, sub):
+        return pl.ds(pl.multiple_of(which * 2 * quarter + sub * quarter, quarter), quarter)
+
     st2 = []
-    for d in range(1, nt):
-        st2.append(rcopy(mine, mine, s_e.at[32 + d], r_e.at[32 + d], tpeer(d), r))
-        st2.append(rcopy(MB.at[t], MB.at[t], s_e.at[40 + d], r_e.at[40 + d], tpeer(d), r))
-    st2.append(rcopy(mine, mine, s_e.at[48], r_e.at[48], t, partner))
-    for cp in st2:
-        cp.start()
-    DP[t, r] = dec_pos[...]
+    for sub in subs:
+        if sub > 0:
+            slots_arrive(sub)
+        E[my_rows, part(core, sub)] = mm(compact, SL[sub].reshape(nr * slots, quarter)).astype(BF16)
+        mine = E.at[my_rows, part(core, sub)]
+        for d in order:
+            st2.append(rcopy(mine, mine, s_e.at[32 + 4 * sub + d], r_e.at[32 + 4 * sub + d], tpeer(d), r))
+            if sub == 0:
+                st2.append(rcopy(MB.at[t], MB.at[t], s_e.at[40 + d], r_e.at[40 + d], tpeer(d), r))
+        st2.append(rcopy(mine, mine, s_e.at[48 + 4 * sub], r_e.at[48 + 4 * sub], t, partner))
+        for cp in st2[-(2 * nt - 1 if sub == 0 else nt):]:
+            cp.start()
 
     def gather(buf, ss, rs):
         hw = dd // 2
@@ -255,7 +273,6 @@
         return step1, step2, step3, finish, drain
 
     g1 = gather(DP, s_g, r_g)
-    g1[0]()
 
     def index_cols(masks):
         ranks = mm(masks.astype(BF16), tri)
@@ -275,18 +292,21 @@
 
     def rows0(vec):
         def take(block, i):
-            got = E.at[blk(block, vis_blk), other_cols]
-            rcopy(got, got, s_e.at[48 + i], r_e.at[48 + i], t, partner).wait_recv()
+            for sub in subs:
+                got = E.at[blk(block, vis_blk), part(1 - core, sub)]
+                rcopy(got, got, s_e.at[48 + 4 * sub + i], r_e.at[48 + 4 * sub + i], t, partner).wait_recv()
             norm_rows(E, A, vis_blk, vec(0), vec(1), block * vis_blk, block * vis_blk)
 
         take(t, 0)
+        for sub in subs:
+            for d in order:
+                got = E.at[blk(tsrc(d), vis_blk), part(core, sub)]
+                rcopy(got, got, s_e.at[32 + 4 * sub + d], r_e.at[32 + 4 * sub + d], t, partner).wait_recv()
+                fw2.append(rcopy(got, got, s_e.at[48 + 4 * sub + d], r_e.at[48 + 4 * sub + d], t, partner))
+                fw2[-1].start()
+        g1[0]()
         for d in order:
-            got = E.at[blk(tsrc(d), vis_blk), my_cols]
-            rcopy(got, got, s_e.at[32 + d], r_e.at[32 + d], t, partner).wait_recv()
-            fw2.append(rcopy(got, got, s_e.at[48 + d], r_e.at[48 + d], t, partner))
-            fw2[-1].start()
             rcopy(MB.at[tsrc(d)], MB.at[tsrc(d)], s_e.at[40 + d], r_e.at[40 + d], t, partner).wait_recv()
-        for d in order:
             take(tsrc(d), d)
 
     def project(dst, rows_n, src_rows, w, w_row, bias):
@@ -468,21 +488,21 @@
 
     start_attention(0, norm(hidden, dvec[0, :1, :], dvec[1, :1, :]))
 
-    def first_rows(d):
+    def first_unit(d):
         tb = tsrc(d)
-        if d > 0:
-            ref = Z.at[tb, :vis_blk]
+        ref = Z.at[tb, :vis_blk]
+
+        @pl.when(d > 0)
+        def _():
             rcopy(ref, ref, s_e.at[56 + d], r_e.at[56 + d], t, partner).wait_recv()
+
         cols_t = IC[tb]
         for q in range(nr):
             u = (mm(one_hot(cols_t[:tok, q:q + 1]), Z[tb]) + DP[tb, q].astype(F32)).astype(BF16)
-            HD[d, q * tok:(q + 1) * tok, :] = norm(u, dvec[0, :1, :], dvec[1, :1, :])
-
-    first_rows(0)
-    for d in range(1, nt):
-        first_rows(d)
-        attend(0, HD[d - 1])
-    attend(0, HD[nt - 1])
+            HD[q * tok:(q + 1) * tok, :] = norm(u, dvec[0, :1, :], dvec[1, :1, :])
+        attend(0, HD[...])
+
+    loop(nt, first_unit)
     hidden = finish_block(0, hidden)
     A2[t, r] = norm(hidden, dvec[0, 1:2, :], dvec[1, 1:2, :])
     H1[:tok, :dd] = hidden
@@ -500,11 +520,13 @@
 
     for d in order:
         g2[1](d)
+    near = [(d, e) for d in order[:2] for e in order[:2]]
+    far = [(d, e) for d in order for e in order if (d, e) not in near]
     unit((0, 0), (1, 0), (3, 0), (0, 1))
+    for d, e in near:
+        g2[2](d, e)
     unit((0, 3), (2, 0), (0, 2))
-    near = [(1, 1), (1, 3), (3, 1), (3, 3)]
-    far = [(1, 2), (2, 1), (2, 3), (3, 2), (2, 2)]
-    for d, e in near + far:
+    for d, e in far:
         g2[2](d, e)
     unit(*near)
     unit(*far)
@@ -534,13 +556,13 @@
         scratch = [pltpu.VMEM(v.shape, v.dtype) for v in small] + [
             pltpu.VMEM((4 * ed, ed), BF16), pltpu.VMEM((4 * ed, ed), BF16),
             pltpu.VMEM((ed, 4 * ed), BF16), pltpu.VMEM((ed, 4 * ed), BF16), pltpu.VMEM((4 * ed, ed), BF16),
-            pltpu.VMEM((CORES, tok // 2, ed // CORES), BF16), pltpu.VMEM((nr, tok // 2, ed // CORES), BF16), pltpu.VMEM((nr, 8, 128), F32), pltpu.VMEM((nt, nr, 128), F32),
+            pltpu.VMEM((4, tok // 2, ed // 4), BF16), pltpu.VMEM((2, nr, tok // 2, ed // 4), BF16), pltpu.VMEM((nr, 8, 128), F32), pltpu.VMEM((nt, nr, 128), F32),
             pltpu.VMEM((nvis, ed), BF16), pltpu.VMEM((nvis // nt, ed), BF16), pltpu.VMEM((nvis // CORES, ed), BF16), pltpu.VMEM((nvis, ed), BF16),
             pltpu.VMEM((nvis, ed), BF16), pltpu.VMEM((nvis // CORES, ed), BF16), pltpu.VMEM((nvis, ed), BF16),
             pltpu.VMEM((ed, nvis), BF16), pltpu.VMEM((nvis // CORES, ed), BF16), pltpu.VMEM((nvis // CORES, 4 * ed), BF16),
             pltpu.VMEM((nt, 128, dd), BF16), pltpu.VMEM((nt, 128, 128), F32),
             pltpu.VMEM((nt, nr, tok, dd), BF16), pltpu.VMEM((nt, nr, tok, dd), BF16),
-            pltpu.VMEM((nt, nr * tok, dd), BF16), pltpu.VMEM((dd // 128, 4 * tok, 128), BF16),
+            pltpu.VMEM((nr * tok, dd), BF16), pltpu.VMEM((dd // 128, 4 * tok, 128), BF16),
             pltpu.VMEM((dd, 4 * tok), F32), pltpu.VMEM((2 * dd // 128, 1, 4 * tok), F32),
         ] + [pltpu.SemaphoreType.DMA((n,)) for n in (16, 24) + (64,) * 6]
         rows = pl.pallas_call(

time: 83.7 us -> 80.9 us (0.967)
  Pallas kernels: 81.5 us -> 78.6 us
    pallas_call x1, Pallas kernels: 81.5 us -> 78.6 us  [local_step(): pl.pallas_call(functools.partial(kernel, nt, nr, len(small)), out_shape=j...]
where the time goes in v4:
time: 80.9 us; the launch traced here: 80.8 us
  Pallas kernels  78.6 us (97%)
  matrix products  2.11 us (3%)
    pallas_call x1, Pallas kernels, local_step(): pl.pallas_call(functools.partial(kernel, nt, nr, len(small)), out_shape=j...  78.6 us
    dot_general x1, matrix products, mm(): return jnp.dot(lhs, rhs, preferred_element_type=F32)  2.11 us

profile of v4, /device:TPU:97, one launch (start us, length us, event | category | flops | bytes accessed | tf_op | source)
XLA Modules:
  0.0 80.8 jit_solution(4507600206753961822)
XLA Ops:
  0.0 78.6 %mae.1 = bf16[64,512]{1,0:T(8,128)(2,1)} custom-call(bf16[64,768]{1,0:T(8,128)(2,1)} %refs_0_.1, bf16[64,1024]{1,0:T(8,128)(2,1)} %refs_1_.1, s32[1,64]{1,0:T(1,128)} %bitcast.23, f32[1,1024]{1,0:T(1,128)} %bitcast.21, bf16[64,512]{1,0:T(8,128)(2,1)} %refs_4_.1, f32[12,2,1024]{2,1,0:T(2,128)} %bitcast.19, f32[2,1024]{1,0:T(2,128)} %refs_6_.1, ...), custom_call_target="tpu_custom_call" | custom-call | tf_op jit(solution)/shard_map/mae/pallas_call | solution.py:568
  78.6 2.1 %fusion = f32[64,768]{1,0:T(8,128)} fusion(bf16[64,512]{1,0:T(8,128)(2,1)} %mae.1, bf16[512,768]{1,0:T(8,128)(2,1)} %param.41), kind=kOutput, calls=%fused_computation | convolution fusion | flops 50331648 | bytes 1048576 | tf_op jit(solution)/shard_map/dot_general | solution.py:20

commit v5 on v4

--- a/solution.py
+++ b/solution.py
@@ -309,31 +309,25 @@
             rcopy(MB.at[tsrc(d)], MB.at[tsrc(d)], s_e.at[40 + d], r_e.at[40 + d], t, partner).wait_recv()
             take(tsrc(d), d)
 
-    def project(dst, rows_n, src_rows, w, w_row, bias):
-        def body(j):
-            cols = blk(j, 512)
-            acc = mm_t(A[src_rows, :], w[pl.ds(pl.multiple_of(w_row + j * 512, 512), 512), :])
-            if bias is not None:
-                acc = acc + bias(cols)
-            dst[:rows_n, cols] = acc.astype(BF16)
-        loop(ed // 512, body)
-
     def enc_layer(layer, w_a, w_up, w_down, src, dst, rows_n, start, dst_start, pairs, wait_rows, wait_down):
         def vec(i):
             return evec[i, layer:layer + 1, :]
 
         wait_rows(vec)
         q_rows = pl.ds(pl.multiple_of(start, rows_n), rows_n)
-        project(Q, rows_n, q_rows, w_a, 0, lambda cols: evec[4, layer:layer + 1, cols])
-        project(K, nvis, slice(None), w_a, ed, None)
-
-        def v_rows(j):
-            rows = blk(j, 512)
-            bias = column_of(evec[5, layer:layer + 1, rows], 128)
-            acc = mm_t(w_a[pl.ds(pl.multiple_of(2 * ed + j * 512, 512), 512), :], A[...])
-            VT[rows, :] = (acc + jnp.concatenate([bias] * (nvis // 128), axis=1)).astype(BF16)
-
-        loop(ed // 512, v_rows)
+
+        def qkv_cols(j):
+            cols = blk(j, 512)
+
+            def w_rows(which):
+                return w_a[pl.ds(pl.multiple_of(which * ed + j * 512, 512), 512), :]
+
+            Q[:rows_n, cols] = (mm_t(A[q_rows, :], w_rows(0)) + evec[4, layer:layer + 1, cols]).astype(BF16)
+            K[:, cols] = mm_t(A[...], w_rows(1)).astype(BF16)
+            bias = column_of(evec[5, layer:layer + 1, cols], 128)
+            VT[cols, :] = (mm_t(w_rows(2), A[...]) + jnp.concatenate([bias] * (nvis // 128), axis=1)).astype(BF16)
+
+        loop(ed // 512, qkv_cols)
 
         def heads2(p):
             for q in range(pairs):
@@ -363,11 +357,11 @@
         o_rows = pl.ds(pl.multiple_of(dst_start, rows_n), rows_n)
 
         def down_cols(j):
-            cols = blk(j, 256)
+            cols = blk(j, 512)
             acc = H1[:rows_n, cols].astype(F32) + mm(HM[:rows_n, :], w_down[:, cols])
             dst[o_rows, cols] = (acc + evec[7, layer:layer + 1, cols]).astype(BF16)
 
-        loop(ed // 256, down_cols)
+        loop(ed // 512, down_cols)
 
     for cp in ld_a:
         cp.wait()
@@ -571,7 +565,7 @@
             in_specs=[pl.BlockSpec(memory_space=pl.ANY)] * (len(small) + len(big)),
             out_specs=pl.BlockSpec(memory_space=pltpu.VMEM),
             scratch_shapes=scratch,
-            compiler_params=pltpu.CompilerParams(collective_id=0, has_side_effects=True, vmem_limit_bytes=64 * 1024 * 1024 - 65536),
+            compiler_params=pltpu.CompilerParams(collective_id=0, has_side_effects=True, vmem_limit_bytes=58 * 1024 * 1024),
             name="mae",
         )(*small, *big)
         return mm(rows, w_out)

time: 80.9 us -> 78.3 us (0.968)
  Pallas kernels: 78.6 us -> 76.3 us
    pallas_call x1, Pallas kernels: 78.6 us -> 76.3 us  [local_step(): pl.pallas_call(functools.partial(kernel, nt, nr, len(small)), out_shape=j...]
where the time goes in v5:
time: 78.3 us; the launch traced here: 78.1 us
  Pallas kernels  76.3 us (97%)
  matrix products  1.78 us (2%)
    pallas_call x1, Pallas kernels, local_step(): pl.pallas_call(functools.partial(kernel, nt, nr, len(small)), out_shape=j...  76.3 us
    dot_general x1, matrix products, mm(): return jnp.dot(lhs, rhs, preferred_element_type=F32)  1.78 us

profile of v5, /device:TPU:97, one launch (start us, length us, event | category | flops | bytes accessed | tf_op | source)
XLA Modules:
  0.0 78.1 jit_solution(651888355564711030)
XLA Ops:
  0.0 0.0 copy-start
  0.0 76.3 %mae.1 = bf16[64,512]{1,0:T(8,128)(2,1)} custom-call(bf16[64,768]{1,0:T(8,128)(2,1)} %refs_0_.1, bf16[64,1024]{1,0:T(8,128)(2,1)} %refs_1_.1, s32[1,64]{1,0:T(1,128)} %bitcast.23, f32[1,1024]{1,0:T(1,128)} %bitcast.21, bf16[64,512]{1,0:T(8,128)(2,1)} %refs_4_.1, f32[12,2,1024]{2,1,0:T(2,128)} %bitcast.19, f32[2,1024]{1,0:T(2,128)} %refs_6_.1, ...), custom_call_target="tpu_custom_call" | custom-call | tf_op jit(solution)/shard_map/mae/pallas_call | solution.py:562
  76.3 0.0 copy-done
  76.3 1.8 %fusion = f32[64,768]{1,0:T(8,128)} fusion(bf16[64,512]{1,0:T(8,128)(2,1)} %mae.1, bf16[512,768]{1,0:T(8,128)(2,1)S(1)} %copy-done), kind=kOutput, calls=%fused_computation | convolution fusion | flops 50331648 | bytes 1048576 | tf_op jit(solution)/shard_map/dot_general | solution.py:20
Async XLA Ops:
  0.0 76.3 %copy-start = (bf16[512,768]{1,0:T(8,128)(2,1)S(1)}, bf16[512,768]{1,0:T(8,128)(2,1)}, u32[]{:S(2)}) copy-start(bf16[512,768]{1,0:T(8,128)(2,1)} %param.41) | copy-start | bytes 2359300
